TPU v7x, 32 devices: a whole 2x2x4 slice. The times are simulated.
32 devices in a mesh: head: 2 (over core), seq: 16 (over z, y, x).
Axes of the slice: x: 2, y: 2, z: 4, core: 2. Of those that a mesh axis runs over, the one named last changes fastest.
Arguments:
- queries: bfloat16 [8192, 4096], P('seq', 'head'), may hold values from -512 to 512
- keys: bfloat16 [8192, 2048], P('seq', 'head'), may hold values from -8 to 8
- values: bfloat16 [8192, 2048], P('seq', 'head'), may hold values from -6 to 6
- episode: int32 [8192], replicated, may hold values from 0 to 7, never falling along the last dimension, each value on 1 to 2048 neighbouring positions
- out_weight: bfloat16 [4096, 4608], P('head'), may hold values from -0.375 to 0.375
Outputs:
- projected: bfloat16 [8192, 4608], P('seq', 'head')
Inputs may be any that keep to these rules, and one draw needn't show every extreme that they name: episode numbers never fall along the trajectory.
All inputs are finite; a program needn't handle non-finite values.
Results may differ from a plain program's by a relative error of at most 0.015.
Values may be sent and summed in bfloat16 or wider, within the bound.
No kernel may reach another device: no remote copies, remote signals or barrier semaphores. Data moves between devices by JAX's collectives and lax.ppermute only.
A program may use at most 256 MiB of HBM per device.

v0:
```python
import math

import jax
import jax.numpy as jnp
from jax import lax
from jax.experimental import pallas as pl
from jax.experimental.pallas import tpu as pltpu
from jax.sharding import PartitionSpec as P


HEAD_DIM = 128
WINDOW = 4096

SCORE_SCALE = math.log2(math.e) / 12.0
HIDDEN = -1e30


def plan(rows, kv_heads, seq_size, tokens):
    reach = min(WINDOW, tokens // 4)
    group = math.gcd(kv_heads, seq_size)
    group &= -group
    while group > 1 and group * rows > reach:
        group //= 2
    before = -(-(reach - 1) // (group * rows))
    back = -(-(reach - 1) // rows)
    return group, before, back


def attend_kernel(chunk, group, before, ratio, rows, meta, qid, kid, *refs):
    n_kv = group * (before + 1)
    far, refs = refs[: 2 * before], refs[2 * before :]
    near, refs = refs[:group], refs[group:]
    q_in, refs = refs[:group], refs[group:]
    outs, refs = refs[:group], refs[group:]
    k_all, v_all, q_all, scores, top, acc = refs
    me = meta[0]
    base = before * group

    def place(ref, row, column, slot):
        at = slice(row, row + rows)
        k_all[slot] = ref[at, column : column + HEAD_DIM]
        v_all[slot, :, :HEAD_DIM] = ref[at, column + HEAD_DIM : column + 2 * HEAD_DIM]

    for p in range(before):
        place(far[2 * p], 0, chunk * 2 * HEAD_DIM, p * group + me)
        for r in range(1, group):
            place(far[2 * p + 1], (r - 1) * rows, 0, p * group + (me ^ r))
    for r in range(group):
        place(near[r], 0, 0, base + (me ^ r))
        q_all[r] = q_in[r][...]
    v_all[:, :, HEAD_DIM:] = jnp.ones((n_kv, rows, HEAD_DIM), jnp.bfloat16)

    def one_block(r, carry):
        at = base + (me ^ r)
        first = meta[1 + r]
        full = meta[1 + group + r]
        top[...] = jnp.full(top.shape, HIDDEN, jnp.float32)
        acc[...] = jnp.zeros(acc.shape, jnp.float32)

        def score(j, masked, diagonal):
            k = k_all[j]
            if masked:
                own = jnp.concatenate([qid[me ^ r]] * (rows // HEAD_DIM), axis=1)
                seen = own == kid[j]
                q_pos = lax.broadcasted_iota(jnp.int32, (rows, rows), 0)
                k_pos = lax.broadcasted_iota(jnp.int32, (rows, rows), 1)
                if diagonal:
                    seen = seen & (k_pos <= q_pos)
                if n_kv * rows > WINDOW or diagonal:
                    seen = seen & (k_pos - q_pos > (at - j) * rows - WINDOW)
            for h in range(ratio):
                q = q_all[r, :, h * HEAD_DIM : (h + 1) * HEAD_DIM]
                s = lax.dot_general(q, k, (((1,), (1,)), ((), ())), preferred_element_type=jnp.float32)
                if masked:
                    s = jnp.where(seen, s, HIDDEN)
                scores[at - j, h] = s
                m = top[h]
                for part in range(rows // HEAD_DIM):
                    m = jnp.maximum(m, s[:, part * HEAD_DIM : (part + 1) * HEAD_DIM])
                top[h] = m

        def masked_step(j, c):
            score(j, True, False)
            return c

        def full_step(j, c):
            score(j, False, False)
            return c

        lax.fori_loop(first, full, masked_step, 0)
        lax.fori_loop(full, at, full_step, 0)
        score(at, True, True)
        for h in range(ratio):
            m = jnp.max(top[h], axis=1, keepdims=True) * SCORE_SCALE
            top[h] = jnp.broadcast_to(m, (rows, HEAD_DIM))

        def mix_step(j, c):
            for h in range(ratio):
                m = jnp.concatenate([top[h]] * (rows // HEAD_DIM), axis=1)
                p = jnp.exp2(scores[at - j, h] * SCORE_SCALE - m).astype(jnp.bfloat16)
                acc[h] += jnp.dot(p, v_all[j], preferred_element_type=jnp.float32)
            return c

        lax.fori_loop(first, at + 1, mix_step, 0)
        for h in range(ratio):
            o = (acc[h, :, :HEAD_DIM] / acc[h, :, HEAD_DIM:]).astype(jnp.bfloat16)
            for n in range(group):

                @pl.when(r == n)
                def _():
                    outs[n][:, h * HEAD_DIM : (h + 1) * HEAD_DIM] = o

        return carry

    lax.fori_loop(0, group, one_block, 0)


def attend(meta, qid, kid, far, near, q, chunk, group, before, back):
    rows = near[0].shape[0]
    width = q[0].shape[1]
    ratio = width // HEAD_DIM
    n_kv = (before + 1) * group
    vmem = pl.BlockSpec(memory_space=pltpu.VMEM)
    return pl.pallas_call(
        lambda *refs: attend_kernel(chunk, group, before, ratio, rows, *refs),
        out_shape=[jax.ShapeDtypeStruct((rows, width), jnp.bfloat16)] * group,
        in_specs=[pl.BlockSpec(memory_space=pltpu.SMEM)] + [vmem] * (2 + len(far) + len(near) + group),
        out_specs=[vmem] * group,
        scratch_shapes=[
            pltpu.VMEM((n_kv, rows, HEAD_DIM), jnp.bfloat16),
            pltpu.VMEM((n_kv, rows, 2 * HEAD_DIM), jnp.bfloat16),
            pltpu.VMEM((group, rows, width), jnp.bfloat16),
            pltpu.VMEM((back + 1, ratio, rows, rows), jnp.float32),
            pltpu.VMEM((ratio, rows, HEAD_DIM), jnp.float32),
            pltpu.VMEM((ratio, rows, 2 * HEAD_DIM), jnp.float32),
        ],
        compiler_params=pltpu.CompilerParams(vmem_limit_bytes=40 << 20),
    )(meta, qid, kid, *far, *near, *q)


def project(me, targets, left, weight, chunk, columns, addends, dtype):
    group = len(left)
    assembled = group == 1
    rows = left[0].shape[-2]
    group, width = left[0].shape[::2] if assembled else (group, left[0].shape[1])
    tile = max(t for t in range(128, 769, 128) if columns % t == 0)
    per = columns // tile
    count = len(targets)
    steps = count * per

    def kernel(info, *refs):
        pieces, refs = refs[: len(left)], refs[len(left) :]
        w, refs = refs[0], refs[1:]
        added, refs = refs[: len(addends)], refs[len(addends) :]
        outs, (w_all, sem) = refs[:-2], refs[-2:]
        lhs = pieces[0] if assembled else outs[-1]

        def fetch(t, n):
            at = pl.ds(pl.multiple_of(info[1 + t] * columns + n * tile, 128), tile)
            row = chunk * group * width
            slot = t * per + n
            return pltpu.make_async_copy(w.at[pl.ds(row, group * width), at], w_all.at[slot], sem.at[slot])

        for t in range(count):
            for n in range(per):
                fetch(t, n).start()
        if not assembled:
            for r in range(group):
                lhs[info[0] ^ r] = pieces[r][...]
        for t in range(count):

            def step(n, carry):
                fetch(t, n).wait()
                here = pl.ds(pl.multiple_of(n * tile, 128), tile)
                wide = jnp.concatenate([lhs[u] for u in range(group)], axis=1)
                total = jnp.dot(wide, w_all[t * per + n], preferred_element_type=jnp.float32)
                if addends:
                    total = total + added[t][:, here]
                outs[t][:, here] = total.astype(dtype)
                return carry

            lax.fori_loop(0, per, step, 0)

    vmem = pl.BlockSpec(memory_space=pltpu.VMEM)
    hbm = pl.BlockSpec(memory_space=pltpu.HBM)
    shapes = [jax.ShapeDtypeStruct((rows, columns), dtype)] * count
    if not assembled:
        shapes.append(jax.ShapeDtypeStruct((group, rows, width), jnp.bfloat16))
    return pl.pallas_call(
        kernel,
        out_shape=shapes,
        in_specs=[pl.BlockSpec(memory_space=pltpu.SMEM)] + [vmem] * len(left) + [hbm] + [vmem] * len(addends),
        out_specs=[vmem] * len(shapes),
        scratch_shapes=[
            pltpu.VMEM((steps, group * width, tile), jnp.bfloat16),
            pltpu.SemaphoreType.DMA((steps,)),
        ],
        compiler_params=pltpu.CompilerParams(vmem_limit_bytes=40 << 20),
    )(jnp.stack([me, *targets]).astype(jnp.int32), *left, weight, *addends)


def add_up(parts):
    rows, columns = parts[0].shape
    tile = max(t for t in range(8, 129, 8) if rows % t == 0)

    def kernel(*refs):
        out, held, sem = refs[-3:]

        def moved(n):
            at = pl.ds(pl.multiple_of(n * tile, 8), tile)
            return pltpu.make_async_copy(held.at[at], out.at[at], sem.at[n])

        def step(n, carry):
            at = pl.ds(pl.multiple_of(n * tile, 8), tile)
            total = refs[0][at].astype(jnp.float32)
            for ref in refs[1:-3]:
                total = total + ref[at].astype(jnp.float32)
            held[at] = total.astype(jnp.bfloat16)
            moved(n).start()
            return carry

        lax.fori_loop(0, rows // tile, step, 0)
        for n in range(rows // tile):
            moved(n).wait()

    return pl.pallas_call(
        kernel,
        out_shape=jax.ShapeDtypeStruct((rows, columns), jnp.bfloat16),
        in_specs=[pl.BlockSpec(memory_space=pltpu.VMEM)] * len(parts),
        out_specs=pl.BlockSpec(memory_space=pltpu.HBM),
        scratch_shapes=[
            pltpu.VMEM((rows, columns), jnp.bfloat16),
            pltpu.SemaphoreType.DMA((rows // tile,)),
        ],
        compiler_params=pltpu.CompilerParams(vmem_limit_bytes=12 << 20),
    )(*parts)


def body(queries, keys, values, episode, out_weight):
    rows = queries.shape[0]
    tokens = episode.shape[0]
    seq_size = lax.axis_size("seq")
    head_size = lax.axis_size("head")
    kv_heads = keys.shape[1] // HEAD_DIM
    ratio = queries.shape[1] // keys.shape[1]
    group, before, back = plan(rows, kv_heads, seq_size, tokens)
    chunks = kv_heads // group
    me = lax.axis_index("seq") % group
    mine = lax.axis_index("seq") // group
    head = lax.axis_index("head")
    n_kv = (before + 1) * group

    def swap(value, r):
        if not r:
            return value
        return lax.ppermute(value, "seq", [(s, s ^ r) for s in range(seq_size)])

    def upward(value, p):
        step = p * group
        return lax.ppermute(value, "seq", [(s, s + step) for s in range(seq_size - step)])

    def columns_of(value, at, heads):
        return lax.dynamic_slice_in_dim(value, at * heads * HEAD_DIM, heads * HEAD_DIM, 1)

    def pair_of(c, r):
        at = c * group + (me ^ r)
        return [columns_of(keys, at, 1), columns_of(values, at, 1)]

    near = [
        [swap(jnp.concatenate(pair_of(c, r), axis=1), r) for r in range(group)]
        for c in range(chunks)
    ]
    own = jnp.concatenate([piece for c in range(chunks) for piece in pair_of(c, 0)], axis=1)
    far_own = [upward(own, p) for p in range(before, 0, -1)]
    own_q = [
        [swap(columns_of(queries, c * group + (me ^ r), ratio), r) for r in range(group)]
        for c in range(chunks)
    ]
    far = []
    for c in range(chunks):
        rest = jnp.concatenate(near[c][1:], axis=0)
        moved = [upward(rest, p) for p in range(before, 0, -1)]
        far.append([piece for pair in zip(far_own, moved) for piece in pair])

    padded = jnp.concatenate([jnp.full((before * group * rows,), -1, jnp.int32), episode])
    ids = lax.dynamic_slice_in_dim(padded, mine * group * rows, n_kv * rows, 0).reshape(n_kv, rows)
    first_id, last_id = ids[:, 0], ids[:, -1]
    at = before * group + (me ^ jnp.arange(group, dtype=jnp.int32))
    first = jnp.sum(last_id[None, :] < jnp.take(first_id, at)[:, None], axis=1, dtype=jnp.int32)
    first = jnp.clip(first, at - back, at)
    full = jnp.sum(first_id[None, :] < jnp.take(last_id, at)[:, None], axis=1, dtype=jnp.int32)
    full = jnp.maximum(full, at + 1 - WINDOW // rows)
    full = jnp.clip(full, first, at)
    meta = jnp.concatenate([me[None].astype(jnp.int32), first, full])
    qid = jnp.broadcast_to(ids[before * group :, :, None], (group, rows, HEAD_DIM))
    kid = ids[:, None, :]

    columns = out_weight.shape[1] // head_size
    targets = [(head + d) % head_size for d in list(range(1, head_size)) + [0]]
    sums = []
    for c in range(chunks):
        mixed = attend(meta, qid, kid, far[c], near[c], own_q[c], c, group, before, back)
        mixed = [swap(piece, r) for r, piece in enumerate(mixed)]
        if c + 1 < chunks:
            *sums, _ = project(me, targets, mixed, out_weight, c, columns, sums, jnp.float32)
    *sent, mixed = project(me, targets[:-1], mixed, out_weight, c, columns, sums[:-1], jnp.bfloat16)
    (kept,) = project(me, targets[-1:], [mixed], out_weight, c, columns, sums[-1:], jnp.bfloat16)
    for d in range(1, head_size):
        ring = [(s, (s + d) % head_size) for s in range(head_size)]
        sent[d - 1] = lax.ppermute(sent[d - 1], "head", ring)
    return add_up([kept, *sent])


def solution(mesh):
    placed = (P("seq", "head"), P("seq", "head"), P("seq", "head"), P(), P("head", None))
    return jax.shard_map(
        body, mesh=mesh, in_specs=placed, out_specs=P("seq", "head"), check_vma=False
    )
```

profile of v0, /device:TPU:13, one launch (start us, length us, event | category | flops | bytes accessed | tf_op | source)
XLA Modules:
  0.0 122.7 jit_solution(1776425200623021410)
XLA Ops:
  0.0 1.8 %constant_dynamic-slice_fusion.8 = (bf16[512,128]{1,0:T(8,128)(2,1)S(1)}, bf16[512,128]{1,0:T(8,128)(2,1)S(1)}, bf16[512,128]{1,0:T(8,128)(2,1)S(1)}, bf16[512,1...) fusion(bf16[512,1024]{1,0:T(8,128)(2,1)} %param.9, ...), kind=kLoop, calls=%fused_computation.23 | loop fusion | bytes 4194336 | tf_op jit(solution)/shard_map/dynamic_slice | solution.py:263
  2.9 2.2 %collective-permute-start.13 = (bf16[512,256]{1,0:T(8,128)(2,1)S(1)}, bf16[512,256]{1,0:T(8,128)(2,1)S(1)}, u32[]{:S(2)}, u32[]{:S(2)}) collective-permute-start(bf16[512,256]{1,0:T(8,128)(2,1)S(1)} %pad_maximum_fusion.9), channel_id=1, source_target_pairs={{0,3},{1,2},{2,1},{3,0},{4,7},{5,6},{6,5},{7,4},{8,11},{9,10},{10,... | collective-permute-start | bytes 786440 | tf_op jit(solution)/shard_map/ppermute | solution.py:256
  5.8 0.7 pad_maximum_fusion.7
  6.5 1.2 collective-permute-start.11
  9.4 0.9 pad_maximum_fusion.2
  10.3 2.6 %constant_dynamic-slice_fusion = (bf16[512,256]{1,0:T(8,128)(2,1)S(1)}, bf16[512,256]{1,0:T(8,128)(2,1)}, bf16[512,256]{1,0:T(8,128)(2,1)S(1)}, bf16[512,256]{1,...) fusion(bf16[512,2048]{1,0:T(8,128)(2,1)} %param.7, ...), kind=kLoop, calls=%fused_computation.15 | loop fusion | bytes 4194336 | tf_op jit(solution)/shard_map/dynamic_slice | solution.py:263
  12.9 2.7 %collective-permute-done.12.refs_7_ = bf16[512,256]{1,0:T(8,128)(2,1)S(1)} collective-permute-done((bf16[512,256]{1,0:T(8,128)(2,1)}, bf16[512,256]{1,0:T(8,128)(2,1)S(1)}, u32[]{:S(2)}, u32[]{:S(2)}) %collective-permute-start.12) | collective-permute-done | bytes 262176 | tf_op jit(solution)/shard_map/ppermute | solution.py:256
  15.7 1.1 collective-permute-start.3
  17.0 1.3 %collective-permute-start.17 = (bf16[512,256]{1,0:T(8,128)(2,1)S(1)}, bf16[512,256]{1,0:T(8,128)(2,1)S(1)}, u32[]{:S(2)}, u32[]{:S(2)}) collective-permute-start(bf16[512,256]{1,0:T(8,128)(2,1)S(1)} %get-tuple-element.32), channel_id=1, source_target_pairs={{0,3},{1,2},{2,1},{3,0},{4,7},{5,6},{6,5},{7,4},{8,11},{9,10},{10,... | collective-permute-start | bytes 786440 | tf_op jit(solution)/shard_map/ppermute | solution.py:256
  18.3 3.8 %collective-permute-done.11.refs_6_ = bf16[512,256]{1,0:T(8,128)(2,1)S(1)} collective-permute-done((bf16[512,256]{1,0:T(8,128)(2,1)}, bf16[512,256]{1,0:T(8,128)(2,1)S(1)}, u32[]{:S(2)}, u32[]{:S(2)}) %collective-permute-start.11) | collective-permute-done | bytes 262176 | tf_op jit(solution)/shard_map/ppermute | solution.py:256
  22.1 1.2 collective-permute-start.15
  23.3 1.0 pad_maximum_fusion.1
  24.3 3.2 %collective-permute-start = (bf16[512,512]{1,0:T(8,128)(2,1)}, bf16[512,512]{1,0:T(8,128)(2,1)S(1)}, u32[]{:S(2)}, u32[]{:S(2)}) collective-permute-start(bf16[512,512]{1,0:T(8,128)(2,1)} %pad_maximum_fusion.2), channel_id=1, source_target_pairs={{0,4},{1,5},{2,6},{3,7},{4,8},{5,9},{6,10},{7,11},{8,12},{9,13},{1... | collective-permute-start | bytes 1572872 | tf_op jit(solution)/shard_map/ppermute | solution.py:260
  27.5 3.2 %collective-permute-start.14 = (bf16[1536,256]{1,0:T(8,128)(2,1)}, bf16[1536,256]{1,0:T(8,128)(2,1)}, u32[]{:S(2)}, u32[]{:S(2)}) collective-permute-start(bf16[1536,256]{1,0:T(8,128)(2,1)} %pad_maximum_fusion.1), channel_id=1, source_target_pairs={{0,4},{1,5},{2,6},{3,7},{4,8},{5,9},{6,10},{7,11},{8,12},{9,13},{1... | collective-permute-start | bytes 2359304 | tf_op jit(solution)/shard_map/ppermute | solution.py:260
  30.7 0.9 pad_maximum_fusion
  31.7 1.9 %collective-permute-start.4 = (bf16[1536,256]{1,0:T(8,128)(2,1)}, bf16[1536,256]{1,0:T(8,128)(2,1)}, u32[]{:S(2)}, u32[]{:S(2)}) collective-permute-start(bf16[1536,256]{1,0:T(8,128)(2,1)} %pad_maximum_fusion), channel_id=1, source_target_pairs={{0,4},{1,5},{2,6},{3,7},{4,8},{5,9},{6,10},{7,11},{8,12},{9,13},{1... | collective-permute-start | bytes 2359304 | tf_op jit(solution)/shard_map/ppermute | solution.py:260
  33.6 0.9 collective-permute-start.16
  34.6 1.0 pad_maximum_fusion.10.refs_5_
  35.6 3.4 %collective-permute-done.15.refs_10_ = bf16[512,256]{1,0:T(8,128)(2,1)S(1)} collective-permute-done((bf16[512,256]{1,0:T(8,128)(2,1)}, bf16[512,256]{1,0:T(8,128)(2,1)S(1)}, u32[]{:S(2)}, u32[]{:S(2)}) %collective-permute-start.15) | collective-permute-done | bytes 262176 | tf_op jit(solution)/shard_map/ppermute | solution.py:256
  39.0 1.2 collective-permute-start.7
  40.1 1.2 %collective-permute-start.6 = (bf16[512,256]{1,0:T(8,128)(2,1)}, bf16[512,256]{1,0:T(8,128)(2,1)}, u32[]{:S(2)}, u32[]{:S(2)}) collective-permute-start(bf16[512,256]{1,0:T(8,128)(2,1)} %get-tuple-element.36), channel_id=1, source_target_pairs={{0,2},{1,3},{2,0},{3,1},{4,6},{5,7},{6,4},{7,5},{8,10},{9,11},{10,... | collective-permute-start | bytes 786440 | tf_op jit(solution)/shard_map/ppermute | solution.py:256
  41.7 11.8 %collective-permute-done.14.refs_4_ = bf16[1536,256]{1,0:T(8,128)(2,1)} collective-permute-done((bf16[1536,256]{1,0:T(8,128)(2,1)}, bf16[1536,256]{1,0:T(8,128)(2,1)}, u32[]{:S(2)}, u32[]{:S(2)}) %collective-permute-start.14) | collective-permute-done | bytes 786464 | tf_op jit(solution)/shard_map/ppermute | solution.py:260
  53.8 0.9 copy-done.1
  54.7 16.5 %shard_map.56 = (bf16[512,256]{1,0:T(8,128)(2,1)S(1)}, bf16[512,256]{1,0:T(8,128)(2,1)S(1)}, bf16[512,256]{1,0:T(8,128)(2,1)}, bf16[512,256]{1,0:T(8,128)(2,1)}) custom-call(s32[9]{0:T(128)S(1)} %pad_add_fusion.2.refs_0_, s32[4,512,128]{2,1,0:T(8,128)S(1)} %broadcast_in_dim.5.refs_1_, s32[8,1,512]{2,1,0:T(1,128)S(1)} %bitcast.4, ...), custom_call_target="tpu_custom_call" | custom-call | tf_op jit(solution)/shard_map/pallas_call | solution.py:124
  71.9 2.1 %collective-permute-start.20 = (bf16[512,256]{1,0:T(8,128)(2,1)}, bf16[512,256]{1,0:T(8,128)(2,1)S(1)}, u32[]{:S(2)}, u32[]{:S(2)}) collective-permute-start(bf16[512,256]{1,0:T(8,128)(2,1)} %get-tuple-element.25), channel_id=1, source_target_pairs={{0,3},{1,2},{2,1},{3,0},{4,7},{5,6},{6,5},{7,4},{8,11},{9,10},{10,... | collective-permute-start | bytes 786440 | tf_op jit(solution)/shard_map/ppermute | solution.py:256
  74.0 16.6 %shard_map.55 = (bf16[512,256]{1,0:T(8,128)(2,1)S(1)}, bf16[512,256]{1,0:T(8,128)(2,1)}, bf16[512,256]{1,0:T(8,128)(2,1)}, bf16[512,256]{1,0:T(8,128)(2,1)S(1)}) custom-call(s32[9]{0:T(128)S(1)} %pad_add_fusion.2.refs_0_, s32[4,512,128]{2,1,0:T(8,128)S(1)} %broadcast_in_dim.5.refs_1_, s32[8,1,512]{2,1,0:T(1,128)S(1)} %bitcast.5, ...), custom_call_target="tpu_custom_call" | custom-call | tf_op jit(solution)/shard_map/pallas_call | solution.py:124
  91.2 2.1 %collective-permute-start.10 = (bf16[512,256]{1,0:T(8,128)(2,1)S(1)}, bf16[512,256]{1,0:T(8,128)(2,1)S(1)}, u32[]{:S(2)}, u32[]{:S(2)}) collective-permute-start(bf16[512,256]{1,0:T(8,128)(2,1)S(1)} %get-tuple-element.21), channel_id=1, source_target_pairs={{0,3},{1,2},{2,1},{3,0},{4,7},{5,6},{6,5},{7,4},{8,11},{9,10},{10,... | collective-permute-start | bytes 786440 | tf_op jit(solution)/shard_map/ppermute | solution.py:256
  93.4 7.9 %shard_map.57 = (f32[512,2304]{1,0:T(8,128)S(1)}, f32[512,2304]{1,0:T(8,128)S(1)}, bf16[4,512,256]{2,1,0:T(8,128)(2,1)}) custom-call(s32[3]{0:T(128)S(1)} %pad_add_fusion.3.info, bf16[512,256]{1,0:T(8,128)(2,1)S(1)} %get-tuple-element.22.refs_0_, bf16[512,256]{1,0:T(8,128)(2,1)S(1)} %collective-permute-done.18.refs_1_, ...), custom_call_target="tpu_custom_call" | custom-call | tf_op jit(solution)/shard_map/pallas_call | solution.py:189
  101.4 5.0 %shard_map.58 = (bf16[512,2304]{1,0:T(8,128)(2,1)S(1)}, bf16[4,512,256]{2,1,0:T(8,128)(2,1)S(1)}) custom-call(s32[2]{0:T(128)S(1)} %pad_add_fusion.1.info, bf16[512,256]{1,0:T(8,128)(2,1)S(1)} %get-tuple-element.18.refs_0_, bf16[512,256]{1,0:T(8,128)(2,1)S(1)} %collective-permute-done.8.refs_1_, bf16[512,256]{1,0:T(8,128)(2,1)S(1)} %collective-permute-done.9.refs_2_, ...), custom_call_target="tpu_custom_call" | custom-call | tf_op jit(solution)/shard_map/pallas_call | solution.py:189
  106.3 9.8 %collective-permute-start.21 = (bf16[512,2304]{1,0:T(8,128)(2,1)S(1)}, bf16[512,2304]{1,0:T(8,128)(2,1)S(1)}, u32[]{:S(2)}, u32[]{:S(2)}) collective-permute-start(bf16[512,2304]{1,0:T(8,128)(2,1)S(1)} %get-tuple-element.29), channel_id=1, source_target_pairs={{0,16},{16,0},{1,17},{17,1},{2,18},{18,2},{3,19},{19,3},{4,20},{20... | collective-permute-start | bytes 7077896 | tf_op jit(solution)/shard_map/ppermute | solution.py:310
  116.2 4.9 %shard_map.59.refs_0_ = bf16[512,2304]{1,0:T(8,128)(2,1)S(1)} custom-call(s32[2]{0:T(128)S(1)} %pad_add_fusion.info, bf16[4,512,256]{2,1,0:T(8,128)(2,1)S(1)} %get-tuple-element.27.refs_0_, bf16[2048,4608]{1,0:T(8,128)(2,1)} %refs_1_.1, f32[512,2304]{1,0:T(8,128)S(1)} %get-tuple-element.28.refs_2_), custom_call_target="tpu_custom_call" | custom-call | tf_op jit(solution)/shard_map/pallas_call | solution.py:189
  121.2 1.6 %shard_map.60 = bf16[512,2304]{1,0:T(8,128)(2,1)} custom-call(bf16[512,2304]{1,0:T(8,128)(2,1)S(1)} %shard_map.59.refs_0_, bf16[512,2304]{1,0:T(8,128)(2,1)S(1)} %collective-permute-done.21.refs_1_), custom_call_target="tpu_custom_call" | custom-call | tf_op jit(solution)/shard_map/pallas_call | solution.py:226
  (67 shorter events, 5.6 us)
Async XLA Ops:
  1.8 7.5 %copy-start.2 = (bf16[512,128]{1,0:T(8,128)(2,1)}, bf16[512,128]{1,0:T(8,128)(2,1)S(1)}, u32[]{:S(2)}) copy-start(bf16[512,128]{1,0:T(8,128)(2,1)S(1)} %get-tuple-element.52) | copy-start | bytes 393220
  1.8 7.5 %copy-start.4 = (bf16[512,128]{1,0:T(8,128)(2,1)}, bf16[512,128]{1,0:T(8,128)(2,1)S(1)}, u32[]{:S(2)}) copy-start(bf16[512,128]{1,0:T(8,128)(2,1)S(1)} %get-tuple-element.63) | copy-start | bytes 393220
  1.8 7.5 %copy-start.6 = (bf16[512,128]{1,0:T(8,128)(2,1)}, bf16[512,128]{1,0:T(8,128)(2,1)S(1)}, u32[]{:S(2)}) copy-start(bf16[512,128]{1,0:T(8,128)(2,1)S(1)} %get-tuple-element.53) | copy-start | bytes 393220
  1.9 7.5 %copy-start.7 = (bf16[512,128]{1,0:T(8,128)(2,1)}, bf16[512,128]{1,0:T(8,128)(2,1)S(1)}, u32[]{:S(2)}) copy-start(bf16[512,128]{1,0:T(8,128)(2,1)S(1)} %get-tuple-element.62) | copy-start | bytes 393220
  1.9 5.9 %copy-start.8 = (s32[8192]{0:T(1024)S(1)}, s32[8192]{0:T(1024)}, u32[]{:S(2)}) copy-start(s32[8192]{0:T(1024)} %param.10) | copy-start | bytes 98308
  2.6 13.0 %collective-permute-start.12 = (bf16[512,256]{1,0:T(8,128)(2,1)}, bf16[512,256]{1,0:T(8,128)(2,1)S(1)}, u32[]{:S(2)}, u32[]{:S(2)}) collective-permute-start(bf16[512,256]{1,0:T(8,128)(2,1)} %pad_maximum_fusion.8), channel_id=1, source_target_pairs={{0,2},{1,3},{2,0},{3,1},{4,6},{5,7},{6,4},{7,5},{8,10},{9,11},{10,... | collective-permute-start | bytes 786440 | tf_op jit(solution)/shard_map/ppermute | solution.py:256
  2.9 14.1 %collective-permute-start.13 = (bf16[512,256]{1,0:T(8,128)(2,1)S(1)}, bf16[512,256]{1,0:T(8,128)(2,1)S(1)}, u32[]{:S(2)}, u32[]{:S(2)}) collective-permute-start(bf16[512,256]{1,0:T(8,128)(2,1)S(1)} %pad_maximum_fusion.9), channel_id=1, source_target_pairs={{0,3},{1,2},{2,1},{3,0},{4,7},{5,6},{6,5},{7,4},{8,11},{9,10},{10,... | collective-permute-start | bytes 786440 | tf_op jit(solution)/shard_map/ppermute | solution.py:256
  5.1 19.2 %collective-permute-start.1 = (bf16[512,256]{1,0:T(8,128)(2,1)S(1)}, bf16[512,256]{1,0:T(8,128)(2,1)S(1)}, u32[]{:S(2)}, u32[]{:S(2)}) collective-permute-start(bf16[512,256]{1,0:T(8,128)(2,1)S(1)} %pad_maximum_fusion.3), channel_id=1, source_target_pairs={{0,1},{1,0},{2,3},{3,2},{4,5},{5,4},{6,7},{7,6},{8,9},{9,8},{10,11... | collective-permute-start | bytes 786440 | tf_op jit(solution)/shard_map/ppermute | solution.py:256
  5.5 22.0 %collective-permute-start.2 = (bf16[512,256]{1,0:T(8,128)(2,1)S(1)}, bf16[512,256]{1,0:T(8,128)(2,1)S(1)}, u32[]{:S(2)}, u32[]{:S(2)}) collective-permute-start(bf16[512,256]{1,0:T(8,128)(2,1)S(1)} %pad_maximum_fusion.4), channel_id=1, source_target_pairs={{0,2},{1,3},{2,0},{3,1},{4,6},{5,7},{6,4},{7,5},{8,10},{9,11},{10,... | collective-permute-start | bytes 786440 | tf_op jit(solution)/shard_map/ppermute | solution.py:256
  6.5 15.6 %collective-permute-start.11 = (bf16[512,256]{1,0:T(8,128)(2,1)}, bf16[512,256]{1,0:T(8,128)(2,1)S(1)}, u32[]{:S(2)}, u32[]{:S(2)}) collective-permute-start(bf16[512,256]{1,0:T(8,128)(2,1)} %pad_maximum_fusion.7), channel_id=1, source_target_pairs={{0,1},{1,0},{2,3},{3,2},{4,5},{5,4},{6,7},{7,6},{8,9},{9,8},{10,11... | collective-permute-start | bytes 786440 | tf_op jit(solution)/shard_map/ppermute | solution.py:256
  15.7 15.1 %collective-permute-start.3 = (bf16[512,256]{1,0:T(8,128)(2,1)S(1)}, bf16[512,256]{1,0:T(8,128)(2,1)S(1)}, u32[]{:S(2)}, u32[]{:S(2)}) collective-permute-start(bf16[512,256]{1,0:T(8,128)(2,1)S(1)} %pad_maximum_fusion.5), channel_id=1, source_target_pairs={{0,3},{1,2},{2,1},{3,0},{4,7},{5,6},{6,5},{7,4},{8,11},{9,10},{10,... | collective-permute-start | bytes 786440 | tf_op jit(solution)/shard_map/ppermute | solution.py:256
  17.0 16.6 %collective-permute-start.17 = (bf16[512,256]{1,0:T(8,128)(2,1)S(1)}, bf16[512,256]{1,0:T(8,128)(2,1)S(1)}, u32[]{:S(2)}, u32[]{:S(2)}) collective-permute-start(bf16[512,256]{1,0:T(8,128)(2,1)S(1)} %get-tuple-element.32), channel_id=1, source_target_pairs={{0,3},{1,2},{2,1},{3,0},{4,7},{5,6},{6,5},{7,4},{8,11},{9,10},{10,... | collective-permute-start | bytes 786440 | tf_op jit(solution)/shard_map/ppermute | solution.py:256
  22.1 16.9 %collective-permute-start.15 = (bf16[512,256]{1,0:T(8,128)(2,1)}, bf16[512,256]{1,0:T(8,128)(2,1)S(1)}, u32[]{:S(2)}, u32[]{:S(2)}) collective-permute-start(bf16[512,256]{1,0:T(8,128)(2,1)} %get-tuple-element.33), channel_id=1, source_target_pairs={{0,1},{1,0},{2,3},{3,2},{4,5},{5,4},{6,7},{7,6},{8,9},{9,8},{10,11... | collective-permute-start | bytes 786440 | tf_op jit(solution)/shard_map/ppermute | solution.py:256
  24.3 17.1 %collective-permute-start = (bf16[512,512]{1,0:T(8,128)(2,1)}, bf16[512,512]{1,0:T(8,128)(2,1)S(1)}, u32[]{:S(2)}, u32[]{:S(2)}) collective-permute-start(bf16[512,512]{1,0:T(8,128)(2,1)} %pad_maximum_fusion.2), channel_id=1, source_target_pairs={{0,4},{1,5},{2,6},{3,7},{4,8},{5,9},{6,10},{7,11},{8,12},{9,13},{1... | collective-permute-start | bytes 1572872 | tf_op jit(solution)/shard_map/ppermute | solution.py:260
  27.5 25.9 %collective-permute-start.14 = (bf16[1536,256]{1,0:T(8,128)(2,1)}, bf16[1536,256]{1,0:T(8,128)(2,1)}, u32[]{:S(2)}, u32[]{:S(2)}) collective-permute-start(bf16[1536,256]{1,0:T(8,128)(2,1)} %pad_maximum_fusion.1), channel_id=1, source_target_pairs={{0,4},{1,5},{2,6},{3,7},{4,8},{5,9},{6,10},{7,11},{8,12},{9,13},{1... | collective-permute-start | bytes 2359304 | tf_op jit(solution)/shard_map/ppermute | solution.py:260
  31.7 42.3 %collective-permute-start.4 = (bf16[1536,256]{1,0:T(8,128)(2,1)}, bf16[1536,256]{1,0:T(8,128)(2,1)}, u32[]{:S(2)}, u32[]{:S(2)}) collective-permute-start(bf16[1536,256]{1,0:T(8,128)(2,1)} %pad_maximum_fusion), channel_id=1, source_target_pairs={{0,4},{1,5},{2,6},{3,7},{4,8},{5,9},{6,10},{7,11},{8,12},{9,13},{1... | collective-permute-start | bytes 2359304 | tf_op jit(solution)/shard_map/ppermute | solution.py:260
  33.6 6.5 %collective-permute-start.16 = (bf16[512,256]{1,0:T(8,128)(2,1)}, bf16[512,256]{1,0:T(8,128)(2,1)}, u32[]{:S(2)}, u32[]{:S(2)}) collective-permute-start(bf16[512,256]{1,0:T(8,128)(2,1)} %get-tuple-element.39), channel_id=1, source_target_pairs={{0,2},{1,3},{2,0},{3,1},{4,6},{5,7},{6,4},{7,5},{8,10},{9,11},{10,... | collective-permute-start | bytes 786440 | tf_op jit(solution)/shard_map/ppermute | solution.py:256
  39.0 14.8 %copy-start = (bf16[512,256]{1,0:T(8,128)(2,1)}, bf16[512,256]{1,0:T(8,128)(2,1)S(1)}, u32[]{:S(2)}) copy-start(bf16[512,256]{1,0:T(8,128)(2,1)S(1)} %collective-permute-done.15.refs_10_) | copy-start | bytes 786436
  39.0 32.6 %collective-permute-start.7 = (bf16[512,256]{1,0:T(8,128)(2,1)}, bf16[512,256]{1,0:T(8,128)(2,1)}, u32[]{:S(2)}, u32[]{:S(2)}) collective-permute-start(bf16[512,256]{1,0:T(8,128)(2,1)} %get-tuple-element.35), channel_id=1, source_target_pairs={{0,3},{1,2},{2,1},{3,0},{4,7},{5,6},{6,5},{7,4},{8,11},{9,10},{10,... | collective-permute-start | bytes 786440 | tf_op jit(solution)/shard_map/ppermute | solution.py:256
  40.1 31.7 %collective-permute-start.6 = (bf16[512,256]{1,0:T(8,128)(2,1)}, bf16[512,256]{1,0:T(8,128)(2,1)}, u32[]{:S(2)}, u32[]{:S(2)}) collective-permute-start(bf16[512,256]{1,0:T(8,128)(2,1)} %get-tuple-element.36), channel_id=1, source_target_pairs={{0,2},{1,3},{2,0},{3,1},{4,6},{5,7},{6,4},{7,5},{8,10},{9,11},{10,... | collective-permute-start | bytes 786440 | tf_op jit(solution)/shard_map/ppermute | solution.py:256
  41.4 32.6 %collective-permute-start.5 = (bf16[512,256]{1,0:T(8,128)(2,1)}, bf16[512,256]{1,0:T(8,128)(2,1)}, u32[]{:S(2)}, u32[]{:S(2)}) collective-permute-start(bf16[512,256]{1,0:T(8,128)(2,1)} %get-tuple-element.37), channel_id=1, source_target_pairs={{0,1},{1,0},{2,3},{3,2},{4,5},{5,4},{6,7},{7,6},{8,9},{9,8},{10,11... | collective-permute-start | bytes 786440 | tf_op jit(solution)/shard_map/ppermute | solution.py:256
  53.8 1.0 copy-start.1
  54.7 16.8 %copy-start.3 = (bf16[512,128]{1,0:T(8,128)(2,1)S(1)}, bf16[512,128]{1,0:T(8,128)(2,1)}, u32[]{:S(2)}) copy-start(bf16[512,128]{1,0:T(8,128)(2,1)} %copy-done.2) | copy-start | bytes 393220
  54.7 16.8 %copy-start.5 = (bf16[512,128]{1,0:T(8,128)(2,1)S(1)}, bf16[512,128]{1,0:T(8,128)(2,1)}, u32[]{:S(2)}) copy-start(bf16[512,128]{1,0:T(8,128)(2,1)} %copy-done.4) | copy-start | bytes 393220
  71.2 20.0 %collective-permute-start.18 = (bf16[512,256]{1,0:T(8,128)(2,1)S(1)}, bf16[512,256]{1,0:T(8,128)(2,1)S(1)}, u32[]{:S(2)}, u32[]{:S(2)}) collective-permute-start(bf16[512,256]{1,0:T(8,128)(2,1)S(1)} %get-tuple-element.23), channel_id=1, source_target_pairs={{0,1},{1,0},{2,3},{3,2},{4,5},{5,4},{6,7},{7,6},{8,9},{9,8},{10,11... | collective-permute-start | bytes 786440 | tf_op jit(solution)/shard_map/ppermute | solution.py:256
  71.5 21.9 %collective-permute-start.19 = (bf16[512,256]{1,0:T(8,128)(2,1)}, bf16[512,256]{1,0:T(8,128)(2,1)S(1)}, u32[]{:S(2)}, u32[]{:S(2)}) collective-permute-start(bf16[512,256]{1,0:T(8,128)(2,1)} %get-tuple-element.24), channel_id=1, source_target_pairs={{0,2},{1,3},{2,0},{3,1},{4,6},{5,7},{6,4},{7,5},{8,10},{9,11},{10,... | collective-permute-start | bytes 786440 | tf_op jit(solution)/shard_map/ppermute | solution.py:256
  71.9 21.6 %collective-permute-start.20 = (bf16[512,256]{1,0:T(8,128)(2,1)}, bf16[512,256]{1,0:T(8,128)(2,1)S(1)}, u32[]{:S(2)}, u32[]{:S(2)}) collective-permute-start(bf16[512,256]{1,0:T(8,128)(2,1)} %get-tuple-element.25), channel_id=1, source_target_pairs={{0,3},{1,2},{2,1},{3,0},{4,7},{5,6},{6,5},{7,4},{8,11},{9,10},{10,... | collective-permute-start | bytes 786440 | tf_op jit(solution)/shard_map/ppermute | solution.py:256
  90.6 10.7 %collective-permute-start.8 = (bf16[512,256]{1,0:T(8,128)(2,1)}, bf16[512,256]{1,0:T(8,128)(2,1)S(1)}, u32[]{:S(2)}, u32[]{:S(2)}) collective-permute-start(bf16[512,256]{1,0:T(8,128)(2,1)} %get-tuple-element.19), channel_id=1, source_target_pairs={{0,1},{1,0},{2,3},{3,2},{4,5},{5,4},{6,7},{7,6},{8,9},{9,8},{10,11... | collective-permute-start | bytes 786440 | tf_op jit(solution)/shard_map/ppermute | solution.py:256
  90.9 10.4 %collective-permute-start.9 = (bf16[512,256]{1,0:T(8,128)(2,1)}, bf16[512,256]{1,0:T(8,128)(2,1)S(1)}, u32[]{:S(2)}, u32[]{:S(2)}) collective-permute-start(bf16[512,256]{1,0:T(8,128)(2,1)} %get-tuple-element.20), channel_id=1, source_target_pairs={{0,2},{1,3},{2,0},{3,1},{4,6},{5,7},{6,4},{7,5},{8,10},{9,11},{10,... | collective-permute-start | bytes 786440 | tf_op jit(solution)/shard_map/ppermute | solution.py:256
  91.2 10.2 %collective-permute-start.10 = (bf16[512,256]{1,0:T(8,128)(2,1)S(1)}, bf16[512,256]{1,0:T(8,128)(2,1)S(1)}, u32[]{:S(2)}, u32[]{:S(2)}) collective-permute-start(bf16[512,256]{1,0:T(8,128)(2,1)S(1)} %get-tuple-element.21), channel_id=1, source_target_pairs={{0,3},{1,2},{2,1},{3,0},{4,7},{5,6},{6,5},{7,4},{8,11},{9,10},{10,... | collective-permute-start | bytes 786440 | tf_op jit(solution)/shard_map/ppermute | solution.py:256
  106.3 14.8 %collective-permute-start.21 = (bf16[512,2304]{1,0:T(8,128)(2,1)S(1)}, bf16[512,2304]{1,0:T(8,128)(2,1)S(1)}, u32[]{:S(2)}, u32[]{:S(2)}) collective-permute-start(bf16[512,2304]{1,0:T(8,128)(2,1)S(1)} %get-tuple-element.29), channel_id=1, source_target_pairs={{0,16},{16,0},{1,17},{17,1},{2,18},{18,2},{3,19},{19,3},{4,20},{20... | collective-permute-start | bytes 7077896 | tf_op jit(solution)/shard_map/ppermute | solution.py:310
where the time goes:
time: 123 us
  Pallas kernels  52.5 us (43%)
  starting transfers between devices  35 us (28%)
  waiting for transfers between devices  21.7 us (18%)
  local copies, waits for them, and re-layouts  7.25 us (6%)
  other arithmetic  5.93 us (5%)
    pallas_call x2, Pallas kernels, attend(): pl.pallas_call(lambda *refs: attend_kernel(chunk, group, before, ratio, r...  33.1 us
    pallas_call x3, Pallas kernels, project(): pl.pallas_call(kernel, out_shape=shapes, in_specs=[pl.BlockSpec(memory_sp...  17.8 us
    ppermute x18, starting transfers between devices, swap(): return lax.ppermute(value, 'seq', [(s, s ^ r) for s in range(seq_size)])  16.9 us
    ppermute x3, waiting for transfers between devices, upward(): lax.ppermute(value, 'seq', [(s, s + step) for s in range(seq_size - step)])  11.8 us
    ppermute x18, waiting for transfers between devices, swap(): return lax.ppermute(value, 'seq', [(s, s ^ r) for s in range(seq_size)])  9.95 us
    ppermute x1, starting transfers between devices, body(): sent[d - 1] = lax.ppermute(sent[d - 1], 'head', ring)  9.8 us
    ppermute x3, starting transfers between devices, upward(): lax.ppermute(value, 'seq', [(s, s + step) for s in range(seq_size - step)])  8.31 us
    dynamic_slice x2, local copies, waits for them, and re-layouts, columns_of(): lax.dynamic_slice_in_dim(value, at * heads * HEAD_DIM, heads * HEAD_DIM, 1)  4.46 us
  transfers between devices with their start and end apart: 22, of which 4 were waited for; matrix products, arithmetic and copies ran while one was open for 8% of the time, Pallas kernels for 37%

commit v1 on v0

v1 whole, which is shorter than its diff:
```python
import math

import jax
import jax.numpy as jnp
from jax import lax
from jax.experimental import pallas as pl
from jax.experimental.pallas import tpu as pltpu
from jax.sharding import PartitionSpec as P


HEAD_DIM = 128
WINDOW = 4096

SCORE_SCALE = math.log2(math.e) / 12.0
HIDDEN = -1e30
ATTEND_ROOM = 16 << 20
PROJECT_ROOM = 26 << 20
SPLIT = False


def plan(rows, kv_heads, seq_size, tokens):
    reach = min(WINDOW, tokens // 4)
    group = math.gcd(kv_heads, seq_size)
    group &= -group
    while group > 1 and group * rows > reach:
        group //= 2
    before = -(-(reach - 1) // (group * rows))
    back = -(-(reach - 1) // rows)
    return group, before, back


def attend_kernel(chunk, group, before, ratio, rows, start, stride, count, meta, qid, kid, *refs):
    n_kv = group * (before + 1)
    far, refs = refs[: 2 * before], refs[2 * before :]
    near, refs = refs[:group], refs[group:]
    q_in, refs = refs[:count], refs[count:]
    outs, refs = refs[:count], refs[count:]
    k_all, v_all, q_all, scores, top, acc = refs
    me = meta[0]
    base = before * group
    cut = rows // 2 if rows % (2 * HEAD_DIM) == 0 else rows

    def place(ref, row, column, slot):
        at = slice(row, row + rows)
        k_all[slot] = ref[at, column : column + HEAD_DIM]
        v_all[slot, :, :HEAD_DIM] = ref[at, column + HEAD_DIM : column + 2 * HEAD_DIM]

    own_column = chunk * 2 * HEAD_DIM
    for p in range(before):
        place(far[2 * p], 0, own_column, p * group + me)
        for r in range(1, group):
            place(far[2 * p + 1], (r - 1) * rows, 0, p * group + (me ^ r))
    for r in range(group):
        place(near[r], 0, 0 if r else own_column, base + (me ^ r))
    for n in range(count):
        q_all[n] = q_in[n][...]
    v_all[:, :, HEAD_DIM:] = jnp.ones((n_kv, rows, HEAD_DIM), jnp.bfloat16)

    def folded(s):
        parts = [s[:, n : n + HEAD_DIM] for n in range(0, s.shape[1], HEAD_DIM)]
        while len(parts) > 1:
            parts = [jnp.maximum(*parts[n : n + 2]) if n + 1 < len(parts) else parts[n] for n in range(0, len(parts), 2)]
        return parts[0]

    def one_block(n, carry):
        r = start + stride * n
        at = base + (me ^ r)
        first = meta[1 + r]
        full = meta[1 + group + r]

        def product(h, low, high, keys):
            q = q_all[n, low:high, h * HEAD_DIM : (h + 1) * HEAD_DIM]
            return lax.dot_general(q, keys, (((1,), (1,)), ((), ())), preferred_element_type=jnp.float32)

        def positions(low, high, wide):
            shape = (high - low, wide)
            q_pos = lax.broadcasted_iota(jnp.int32, shape, 0) + low
            return q_pos, lax.broadcasted_iota(jnp.int32, shape, 1)

        def same_episode(j, low, high, wide):
            own = jnp.concatenate([qid[me ^ r, low:high]] * (wide // HEAD_DIM), axis=1)
            return own == kid[j, :, :wide]

        for low in range(0, rows, cut):
            high = low + cut
            q_pos, k_pos = positions(low, high, high)
            seen = same_episode(at, low, high, high) & (k_pos <= q_pos)
            if rows > WINDOW:
                seen = seen & (k_pos - q_pos > -WINDOW)
            for h in range(ratio):
                s = jnp.where(seen, product(h, low, high, k_all[at, :high]), HIDDEN)
                scores[0, h, low:high, :high] = s
                top[h, low:high] = folded(s)

        def score(j, masked):
            keys = k_all[j]
            if masked:
                seen = same_episode(j, 0, rows, rows)
                if n_kv * rows > WINDOW:
                    q_pos, k_pos = positions(0, rows, rows)
                    seen = seen & (k_pos - q_pos > (at - j) * rows - WINDOW)
            for h in range(ratio):
                s = product(h, 0, rows, keys)
                if masked:
                    s = jnp.where(seen, s, HIDDEN)
                scores[at - j, h] = s
                top[h] = jnp.maximum(top[h], folded(s))

        def masked_step(j, c):
            score(j, True)
            return c

        def full_step(j, c):
            score(j, False)
            return c

        lax.fori_loop(first, full, masked_step, 0)
        lax.fori_loop(full, at, full_step, 0)
        for h in range(ratio):
            m = jnp.max(top[h], axis=1, keepdims=True) * SCORE_SCALE
            top[h] = jnp.broadcast_to(m, (rows, HEAD_DIM))

        def weighted(j, h, low, high, wide):
            m = jnp.concatenate([top[h, low:high]] * (wide // HEAD_DIM), axis=1)
            p = jnp.exp2(scores[at - j, h, low:high, :wide] * SCORE_SCALE - m).astype(jnp.bfloat16)
            return jnp.dot(p, v_all[j, :wide], preferred_element_type=jnp.float32)

        for h in range(ratio):
            for low in range(0, rows, cut):
                acc[h, low : low + cut] = weighted(at, h, low, low + cut, low + cut)

        def mix_step(j, c):
            for h in range(ratio):
                acc[h] += weighted(j, h, 0, rows, rows)
            return c

        lax.fori_loop(first, at, mix_step, 0)
        for h in range(ratio):
            o = (acc[h, :, :HEAD_DIM] / acc[h, :, HEAD_DIM:]).astype(jnp.bfloat16)
            for k in range(count):

                @pl.when(n == k)
                def _():
                    outs[k][:, h * HEAD_DIM : (h + 1) * HEAD_DIM] = o

        return carry

    lax.fori_loop(0, count, one_block, 0)


def attend(meta, qid, kid, far, near, q, chunk, group, before, back, start, stride):
    rows, width = q[0].shape
    ratio = width // HEAD_DIM
    n_kv = (before + 1) * group
    count = len(q)
    vmem = pl.BlockSpec(memory_space=pltpu.VMEM)
    tiles = (back + 1) * ratio * rows * rows * 4
    return pl.pallas_call(
        lambda *refs: attend_kernel(chunk, group, before, ratio, rows, start, stride, count, *refs),
        out_shape=[jax.ShapeDtypeStruct((rows, width), jnp.bfloat16)] * count,
        in_specs=[pl.BlockSpec(memory_space=pltpu.SMEM)] + [vmem] * (2 + len(far) + len(near) + count),
        out_specs=[vmem] * count,
        scratch_shapes=[
            pltpu.VMEM((n_kv, rows, HEAD_DIM), jnp.bfloat16),
            pltpu.VMEM((n_kv, rows, 2 * HEAD_DIM), jnp.bfloat16),
            pltpu.VMEM((count, rows, width), jnp.bfloat16),
            pltpu.VMEM((back + 1, ratio, rows, rows), jnp.float32),
            pltpu.VMEM((ratio, rows, HEAD_DIM), jnp.float32),
            pltpu.VMEM((ratio, rows, 2 * HEAD_DIM), jnp.float32),
        ],
        compiler_params=pltpu.CompilerParams(vmem_limit_bytes=tiles + ATTEND_ROOM),
    )(meta, qid, kid, *far, *near, *q)


def project(me, targets, left, weight, chunk, columns, addends, dtype, ahead=None, ready=()):
    assembled = len(left) == 1
    group, rows, width = left[0].shape if assembled else (len(left), *left[0].shape)
    depth = group * width
    tile = max(t for t in range(128, 769, 128) if columns % t == 0)
    per = columns // tile
    count = len(targets)
    steps = count * per
    more = count if ahead is not None else 0

    def kernel(info, *refs):
        pieces, refs = refs[: len(left)], refs[len(left) :]
        w, refs = refs[: max(1, len(ready))], refs[max(1, len(ready)) :]
        added, refs = refs[: len(addends)], refs[len(addends) :]
        outs, (w_all, sem, sem_ahead) = refs[:-3], refs[-3:]
        lhs = pieces[0] if assembled else outs[count]

        def fetch(t, n):
            at = pl.ds(pl.multiple_of(info[1 + t] * columns + n * tile, 128), tile)
            slot = t * per + n
            source = w[0].at[pl.ds(chunk * depth, depth), at]
            return pltpu.make_async_copy(source, w_all.at[slot], sem.at[slot])

        def fetch_ahead(t):
            at = pl.ds(pl.multiple_of(info[1 + t] * columns, 128), columns)
            source = w[0].at[pl.ds(ahead * depth, depth), at]
            return pltpu.make_async_copy(source, outs[len(outs) - more + t], sem_ahead.at[t])

        if not ready:
            for t in range(count):
                for n in range(per):
                    fetch(t, n).start()
        for t in range(more):
            fetch_ahead(t).start()
        if not assembled:
            for r in range(group):
                lhs[info[0] ^ r] = pieces[r][...]
        for t in range(count):

            def step(n, carry):
                here = pl.ds(pl.multiple_of(n * tile, 128), tile)
                if ready:
                    w_tile = w[t][:, here]
                else:
                    fetch(t, n).wait()
                    w_tile = w_all[t * per + n]
                wide = jnp.concatenate([lhs[u] for u in range(group)], axis=1)
                total = jnp.dot(wide, w_tile, preferred_element_type=jnp.float32)
                if addends:
                    total = total + added[t][:, here]
                outs[t][:, here] = total.astype(dtype)
                return carry

            lax.fori_loop(0, per, step, 0)
        for t in range(more):
            fetch_ahead(t).wait()

    vmem = pl.BlockSpec(memory_space=pltpu.VMEM)
    hbm = pl.BlockSpec(memory_space=pltpu.HBM)
    shapes = [jax.ShapeDtypeStruct((rows, columns), dtype)] * count
    if not assembled:
        shapes.append(jax.ShapeDtypeStruct((group, rows, width), jnp.bfloat16))
    shapes += [jax.ShapeDtypeStruct((depth, columns), jnp.bfloat16)] * more
    return pl.pallas_call(
        kernel,
        out_shape=shapes,
        in_specs=[pl.BlockSpec(memory_space=pltpu.SMEM)]
        + [vmem] * len(left)
        + ([vmem] * len(ready) or [hbm])
        + [vmem] * len(addends),
        out_specs=[vmem] * len(shapes),
        scratch_shapes=[
            pltpu.VMEM((1, 16, 128) if ready else (steps, depth, tile), jnp.bfloat16),
            pltpu.SemaphoreType.DMA((steps,)),
            pltpu.SemaphoreType.DMA((max(1, more),)),
        ],
        compiler_params=pltpu.CompilerParams(vmem_limit_bytes=PROJECT_ROOM),
    )(jnp.stack([me, *targets]).astype(jnp.int32), *left, *(ready or [weight]), *addends)


def add_up(parts):
    rows, columns = parts[0].shape
    tile = max(t for t in range(8, 129, 8) if rows % t == 0)

    def kernel(*refs):
        out, held, sem = refs[-3:]

        def moved(n):
            at = pl.ds(pl.multiple_of(n * tile, 8), tile)
            return pltpu.make_async_copy(held.at[at], out.at[at], sem.at[n])

        def step(n, carry):
            at = pl.ds(pl.multiple_of(n * tile, 8), tile)
            total = refs[0][at].astype(jnp.float32)
            for ref in refs[1:-3]:
                total = total + ref[at].astype(jnp.float32)
            held[at] = total.astype(jnp.bfloat16)
            moved(n).start()
            return carry

        lax.fori_loop(0, rows // tile, step, 0)
        for n in range(rows // tile):
            moved(n).wait()

    return pl.pallas_call(
        kernel,
        out_shape=jax.ShapeDtypeStruct((rows, columns), jnp.bfloat16),
        in_specs=[pl.BlockSpec(memory_space=pltpu.VMEM)] * len(parts),
        out_specs=pl.BlockSpec(memory_space=pltpu.HBM),
        scratch_shapes=[
            pltpu.VMEM((rows, columns), jnp.bfloat16),
            pltpu.SemaphoreType.DMA((rows // tile,)),
        ],
        compiler_params=pltpu.CompilerParams(vmem_limit_bytes=12 << 20),
    )(*parts)


def body(queries, keys, values, episode, out_weight):
    rows = queries.shape[0]
    tokens = episode.shape[0]
    seq_size = lax.axis_size("seq")
    head_size = lax.axis_size("head")
    kv_heads = keys.shape[1] // HEAD_DIM
    ratio = queries.shape[1] // keys.shape[1]
    group, before, back = plan(rows, kv_heads, seq_size, tokens)
    chunks = kv_heads // group
    me = lax.axis_index("seq") % group
    mine = lax.axis_index("seq") // group
    head = lax.axis_index("head")
    n_kv = (before + 1) * group

    def swap(value, r):
        if not r:
            return value
        return lax.ppermute(value, "seq", [(s, s ^ r) for s in range(seq_size)])

    def upward(value, p):
        step = p * group
        return lax.ppermute(value, "seq", [(s, s + step) for s in range(seq_size - step)])

    def columns_of(value, at, heads):
        return lax.dynamic_slice_in_dim(value, at * heads * HEAD_DIM, heads * HEAD_DIM, 1)

    def pair_of(c, r):
        at = c * group + (me ^ r)
        return [columns_of(keys, at, 1), columns_of(values, at, 1)]

    own = jnp.concatenate([piece for c in range(chunks) for piece in pair_of(c, 0)], axis=1)
    near = [[own] + [swap(jnp.concatenate(pair_of(c, r), axis=1), r) for r in range(1, group)] for c in range(chunks)]
    far_own = [upward(own, p) for p in range(before, 0, -1)]
    own_q = [[swap(columns_of(queries, c * group + (me ^ r), ratio), r) for r in range(group)] for c in range(chunks)]
    far = []
    for c in range(chunks):
        rest = jnp.concatenate(near[c][1:], axis=0)
        moved = [upward(rest, p) for p in range(before, 0, -1)]
        far.append([piece for pair in zip(far_own, moved) for piece in pair])

    padded = jnp.concatenate([jnp.full((before * group * rows,), -1, jnp.int32), episode])
    ids = lax.dynamic_slice_in_dim(padded, mine * group * rows, n_kv * rows, 0).reshape(n_kv, rows)
    first_id, last_id = ids[:, 0], ids[:, -1]
    at = before * group + (me ^ jnp.arange(group, dtype=jnp.int32))
    first = jnp.sum(last_id[None, :] < jnp.take(first_id, at)[:, None], axis=1, dtype=jnp.int32)
    first = jnp.clip(first, at - back, at)
    full = jnp.sum(first_id[None, :] < jnp.take(last_id, at)[:, None], axis=1, dtype=jnp.int32)
    full = jnp.maximum(full, at + 1 - WINDOW // rows)
    full = jnp.clip(full, first, at)
    meta = jnp.concatenate([me[None].astype(jnp.int32), first, full])
    qid = jnp.broadcast_to(ids[before * group :, :, None], (group, rows, HEAD_DIM))
    kid = ids[:, None, :]

    columns = out_weight.shape[1] // head_size
    targets = [(head + d) % head_size for d in list(range(1, head_size)) + [0]]
    sums, ready = [], []
    for c in range(chunks):
        mixed = [None] * group
        stride = 2 if SPLIT and group > 1 and c + 1 == chunks else 1
        for start in range(stride - 1, -1, -1):
            done = attend(
                meta, qid, kid, far[c], near[c], own_q[c][start::stride], c, group, before, back, start, stride
            )
            for r, piece in zip(range(start, group, stride), done):
                mixed[r] = swap(piece, r)
        if c + 1 < chunks:
            ahead = c + 1 if c + 2 == chunks else None
            made = project(me, targets, mixed, out_weight, c, columns, sums, jnp.float32, ahead)
            sums, ready = made[:head_size], made[head_size + 1 :]
    *sent, mixed = project(
        me, targets[:-1], mixed, out_weight, c, columns, sums[:-1], jnp.bfloat16, None, ready[:-1]
    )
    (kept,) = project(
        me, targets[-1:], [mixed], out_weight, c, columns, sums[-1:], jnp.bfloat16, None, ready[-1:]
    )
    for d in range(1, head_size):
        ring = [(s, (s + d) % head_size) for s in range(head_size)]
        sent[d - 1] = lax.ppermute(sent[d - 1], "head", ring)
    return add_up([kept, *sent])


def solution(mesh):
    placed = (P("seq", "head"), P("seq", "head"), P("seq", "head"), P(), P("head", None))
    return jax.shard_map(body, mesh=mesh, in_specs=placed, out_specs=P("seq", "head"), check_vma=False)
```

time: 123 us -> 120 us (0.976)
  the two profiles are of different devices: /device:TPU:13 before, /device:TPU:9 now
where the time goes in v1:
time: 120 us; the launch traced here: 119 us
  Pallas kernels  48.7 us (41%)
  starting transfers between devices  35.8 us (30%)
  waiting for transfers between devices  22.6 us (19%)
  local copies, waits for them, and re-layouts  7.21 us (6%)
  other arithmetic  4.76 us (4%)
    pallas_call x2, Pallas kernels, attend(): pl.pallas_call(lambda *refs: attend_kernel(chunk, group, before, ratio, r...  31 us
    ppermute x18, starting transfers between devices, swap(): return lax.ppermute(value, 'seq', [(s, s ^ r) for s in range(seq_size)])  17.6 us
    pallas_call x3, Pallas kernels, project(): pl.pallas_call(kernel, out_shape=shapes, in_specs=[pl.BlockSpec(memory_sp...  16.1 us
    ppermute x3, waiting for transfers between devices, upward(): lax.ppermute(value, 'seq', [(s, s + step) for s in range(seq_size - step)])  11.4 us
    ppermute x18, waiting for transfers between devices, swap(): return lax.ppermute(value, 'seq', [(s, s ^ r) for s in range(seq_size)])  10.7 us
    ppermute x1, starting transfers between devices, body(): sent[d - 1] = lax.ppermute(sent[d - 1], 'head', ring)  9.88 us
    ppermute x3, starting transfers between devices, upward(): lax.ppermute(value, 'seq', [(s, s + step) for s in range(seq_size - step)])  8.31 us
    dynamic_slice x2, local copies, waits for them, and re-layouts, columns_of(): lax.dynamic_slice_in_dim(value, at * heads * HEAD_DIM, heads * HEAD_DIM, 1)  4.44 us
  transfers between devices with their start and end apart: 22, of which 6 were waited for; matrix products, arithmetic and copies ran while one was open for 8% of the time, Pallas kernels for 36%

profile of v1, /device:TPU:9, one launch (start us, length us, event | category | flops | bytes accessed | tf_op | source)
XLA Modules:
  0.0 119.4 jit_solution(12292137880959124397)
XLA Ops:
  0.0 1.8 %constant_dynamic-slice_fusion.8 = (bf16[512,128]{1,0:T(8,128)(2,1)S(1)}, bf16[512,128]{1,0:T(8,128)(2,1)S(1)}, bf16[512,128]{1,0:T(8,128)(2,1)S(1)}, bf16[512,1...) fusion(bf16[512,1024]{1,0:T(8,128)(2,1)} %param.9, ...), kind=kLoop, calls=%fused_computation.21 | loop fusion | bytes 4194336 | tf_op jit(solution)/shard_map/dynamic_slice | solution.py:316
  1.9 1.3 %collective-permute-start.12 = (bf16[512,256]{1,0:T(8,128)(2,1)S(1)}, bf16[512,256]{1,0:T(8,128)(2,1)S(1)}, u32[]{:S(2)}, u32[]{:S(2)}) collective-permute-start(bf16[512,256]{1,0:T(8,128)(2,1)S(1)} %pad_maximum_fusion.7), channel_id=1, source_target_pairs={{0,2},{1,3},{2,0},{3,1},{4,6},{5,7},{6,4},{7,5},{8,10},{9,11},{10,... | collective-permute-start | bytes 786440 | tf_op jit(solution)/shard_map/ppermute | solution.py:309
  3.9 1.2 collective-permute-start.13
  5.4 0.7 pad_maximum_fusion.4
  6.1 1.2 %collective-permute-start.2 = (bf16[512,256]{1,0:T(8,128)(2,1)}, bf16[512,256]{1,0:T(8,128)(2,1)S(1)}, u32[]{:S(2)}, u32[]{:S(2)}) collective-permute-start(bf16[512,256]{1,0:T(8,128)(2,1)} %pad_maximum_fusion.4), channel_id=1, source_target_pairs={{0,2},{1,3},{2,0},{3,1},{4,6},{5,7},{6,4},{7,5},{8,10},{9,11},{10,... | collective-permute-start | bytes 786440 | tf_op jit(solution)/shard_map/ppermute | solution.py:309
  8.1 1.2 %collective-permute-start.11 = (bf16[512,256]{1,0:T(8,128)(2,1)}, bf16[512,256]{1,0:T(8,128)(2,1)S(1)}, u32[]{:S(2)}, u32[]{:S(2)}) collective-permute-start(bf16[512,256]{1,0:T(8,128)(2,1)} %pad_maximum_fusion.6), channel_id=1, source_target_pairs={{0,1},{1,0},{2,3},{3,2},{4,5},{5,4},{6,7},{7,6},{8,9},{9,8},{10,11... | collective-permute-start | bytes 786440 | tf_op jit(solution)/shard_map/ppermute | solution.py:309
  10.9 2.6 %constant_dynamic-slice_fusion = (bf16[512,256]{1,0:T(8,128)(2,1)S(1)}, bf16[512,256]{1,0:T(8,128)(2,1)}, bf16[512,256]{1,0:T(8,128)(2,1)S(1)}, bf16[512,256]{1,...) fusion(bf16[512,2048]{1,0:T(8,128)(2,1)} %param.7, ...), kind=kLoop, calls=%fused_computation.13 | loop fusion | bytes 4194336 | tf_op jit(solution)/shard_map/dynamic_slice | solution.py:316
  13.6 1.2 collective-permute-done.12.refs_7_
  14.7 2.2 %collective-permute-start.3 = (bf16[512,256]{1,0:T(8,128)(2,1)S(1)}, bf16[512,256]{1,0:T(8,128)(2,1)S(1)}, u32[]{:S(2)}, u32[]{:S(2)}) collective-permute-start(bf16[512,256]{1,0:T(8,128)(2,1)S(1)} %pad_maximum_fusion.5), channel_id=1, source_target_pairs={{0,3},{1,2},{2,1},{3,0},{4,7},{5,6},{6,5},{7,4},{8,11},{9,10},{10,... | collective-permute-start | bytes 786440 | tf_op jit(solution)/shard_map/ppermute | solution.py:309
  17.2 5.1 %collective-permute-done.11.refs_6_ = bf16[512,256]{1,0:T(8,128)(2,1)S(1)} collective-permute-done((bf16[512,256]{1,0:T(8,128)(2,1)}, bf16[512,256]{1,0:T(8,128)(2,1)S(1)}, u32[]{:S(2)}, u32[]{:S(2)}) %collective-permute-start.11) | collective-permute-done | bytes 262176 | tf_op jit(solution)/shard_map/ppermute | solution.py:309
  22.3 1.2 %collective-permute-start.15 = (bf16[512,256]{1,0:T(8,128)(2,1)}, bf16[512,256]{1,0:T(8,128)(2,1)}, u32[]{:S(2)}, u32[]{:S(2)}) collective-permute-start(bf16[512,256]{1,0:T(8,128)(2,1)} %get-tuple-element.37), channel_id=1, source_target_pairs={{0,1},{1,0},{2,3},{3,2},{4,5},{5,4},{6,7},{7,6},{8,9},{9,8},{10,11... | collective-permute-start | bytes 786440 | tf_op jit(solution)/shard_map/ppermute | solution.py:309
  23.5 0.9 pad_maximum_fusion.1
  24.4 3.2 %collective-permute-start = (bf16[512,512]{1,0:T(8,128)(2,1)S(1)}, bf16[512,512]{1,0:T(8,128)(2,1)S(1)}, u32[]{:S(2)}, u32[]{:S(2)}) collective-permute-start(bf16[512,512]{1,0:T(8,128)(2,1)S(1)} %pad_maximum_fusion.2.refs_5_), channel_id=1, source_target_pairs={{0,4},{1,5},{2,6},{3,7},{4,8},{5,9},{6,10},{7,11},{8,12},{9,13},{1... | collective-permute-start | bytes 1572872 | tf_op jit(solution)/shard_map/ppermute | solution.py:313
  27.7 3.2 %collective-permute-start.14 = (bf16[1536,256]{1,0:T(8,128)(2,1)}, bf16[1536,256]{1,0:T(8,128)(2,1)}, u32[]{:S(2)}, u32[]{:S(2)}) collective-permute-start(bf16[1536,256]{1,0:T(8,128)(2,1)} %pad_maximum_fusion.1), channel_id=1, source_target_pairs={{0,4},{1,5},{2,6},{3,7},{4,8},{5,9},{6,10},{7,11},{8,12},{9,13},{1... | collective-permute-start | bytes 2359304 | tf_op jit(solution)/shard_map/ppermute | solution.py:313
  30.9 0.9 pad_maximum_fusion
  31.8 1.9 %collective-permute-start.4 = (bf16[1536,256]{1,0:T(8,128)(2,1)}, bf16[1536,256]{1,0:T(8,128)(2,1)}, u32[]{:S(2)}, u32[]{:S(2)}) collective-permute-start(bf16[1536,256]{1,0:T(8,128)(2,1)} %pad_maximum_fusion), channel_id=1, source_target_pairs={{0,4},{1,5},{2,6},{3,7},{4,8},{5,9},{6,10},{7,11},{8,12},{9,13},{1... | collective-permute-start | bytes 2359304 | tf_op jit(solution)/shard_map/ppermute | solution.py:313
  34.5 0.8 collective-permute-start.16
  35.4 3.9 %collective-permute-done.15.refs_10_ = bf16[512,256]{1,0:T(8,128)(2,1)} collective-permute-done((bf16[512,256]{1,0:T(8,128)(2,1)}, bf16[512,256]{1,0:T(8,128)(2,1)}, u32[]{:S(2)}, u32[]{:S(2)}) %collective-permute-start.15) | collective-permute-done | bytes 262176 | tf_op jit(solution)/shard_map/ppermute | solution.py:309
  39.3 2.2 %collective-permute-start.7 = (bf16[512,256]{1,0:T(8,128)(2,1)}, bf16[512,256]{1,0:T(8,128)(2,1)}, u32[]{:S(2)}, u32[]{:S(2)}) collective-permute-start(bf16[512,256]{1,0:T(8,128)(2,1)} %get-tuple-element.39), channel_id=1, source_target_pairs={{0,3},{1,2},{2,1},{3,0},{4,7},{5,6},{6,5},{7,4},{8,11},{9,10},{10,... | collective-permute-start | bytes 786440 | tf_op jit(solution)/shard_map/ppermute | solution.py:309
  41.9 11.4 %collective-permute-done.14.refs_4_ = bf16[1536,256]{1,0:T(8,128)(2,1)} collective-permute-done((bf16[1536,256]{1,0:T(8,128)(2,1)}, bf16[1536,256]{1,0:T(8,128)(2,1)}, u32[]{:S(2)}, u32[]{:S(2)}) %collective-permute-start.14) | collective-permute-done | bytes 786464 | tf_op jit(solution)/shard_map/ppermute | solution.py:313
  53.7 0.9 copy-done.1
  54.7 15.4 %shard_map.56 = (bf16[512,256]{1,0:T(8,128)(2,1)S(1)}, bf16[512,256]{1,0:T(8,128)(2,1)S(1)}, bf16[512,256]{1,0:T(8,128)(2,1)}, bf16[512,256]{1,0:T(8,128)(2,1)}) custom-call(s32[9]{0:T(128)S(1)} %pad_add_fusion.2.refs_0_, s32[4,512,128]{2,1,0:T(8,128)S(1)} %broadcast_in_dim.5.refs_1_, s32[8,1,512]{2,1,0:T(1,128)S(1)} %bitcast.4, ...), custom_call_target="tpu_custom_call" | custom-call | tf_op jit(solution)/shard_map/pallas_call | solution.py:158
  70.3 1.2 %collective-permute-start.19 = (bf16[512,256]{1,0:T(8,128)(2,1)}, bf16[512,256]{1,0:T(8,128)(2,1)S(1)}, u32[]{:S(2)}, u32[]{:S(2)}) collective-permute-start(bf16[512,256]{1,0:T(8,128)(2,1)} %get-tuple-element.26), channel_id=1, source_target_pairs={{0,2},{1,3},{2,0},{3,1},{4,6},{5,7},{6,4},{7,5},{8,10},{9,11},{10,... | collective-permute-start | bytes 786440 | tf_op jit(solution)/shard_map/ppermute | solution.py:309
  71.6 1.2 collective-permute-start.20
  72.7 15.6 %shard_map.55 = (bf16[512,256]{1,0:T(8,128)(2,1)S(1)}, bf16[512,256]{1,0:T(8,128)(2,1)}, bf16[512,256]{1,0:T(8,128)(2,1)}, bf16[512,256]{1,0:T(8,128)(2,1)}) custom-call(s32[9]{0:T(128)S(1)} %pad_add_fusion.2.refs_0_, s32[4,512,128]{2,1,0:T(8,128)S(1)} %broadcast_in_dim.5.refs_1_, s32[8,1,512]{2,1,0:T(1,128)S(1)} %bitcast.5, ...), custom_call_target="tpu_custom_call" | custom-call | tf_op jit(solution)/shard_map/pallas_call | solution.py:158
  88.6 1.2 %collective-permute-start.9 = (bf16[512,256]{1,0:T(8,128)(2,1)}, bf16[512,256]{1,0:T(8,128)(2,1)S(1)}, u32[]{:S(2)}, u32[]{:S(2)}) collective-permute-start(bf16[512,256]{1,0:T(8,128)(2,1)} %get-tuple-element.22), channel_id=1, source_target_pairs={{0,2},{1,3},{2,0},{3,1},{4,6},{5,7},{6,4},{7,5},{8,10},{9,11},{10,... | collective-permute-start | bytes 786440 | tf_op jit(solution)/shard_map/ppermute | solution.py:309
  89.8 1.2 collective-permute-start.10
  91.2 8.9 %shard_map.57 = (f32[512,2304]{1,0:T(8,128)S(1)}, f32[512,2304]{1,0:T(8,128)S(1)}, bf16[4,512,256]{2,1,0:T(8,128)(2,1)}, bf16[1024,2304]{1,0:T(8,128)(2,1)S(1)}, bf16[1024,2304]{1,0:T(8,128)(2,1)S(1)}) custom-call(s32[3]{0:T(128)S(1)} %pad_add_fusion.3.info, bf16[512,256]{1,0:T(8,128)(2,1)S(1)} %get-tuple-element.24.refs_0_, ...), custom_call_target="tpu_custom_call" | custom-call | tf_op jit(solution)/shard_map/pallas_call | solution.py:238
  100.1 3.6 %shard_map.58 = (bf16[512,2304]{1,0:T(8,128)(2,1)S(1)}, bf16[4,512,256]{2,1,0:T(8,128)(2,1)S(1)}) custom-call(s32[2]{0:T(128)S(1)} %pad_add_fusion.1.info, bf16[512,256]{1,0:T(8,128)(2,1)S(1)} %get-tuple-element.20.refs_0_, bf16[512,256]{1,0:T(8,128)(2,1)S(1)} %collective-permute-done.8.refs_1_, bf16[512,256]{1,0:T(8,128)(2,1)S(1)} %collective-permute-done.9.refs_2_, ...), custom_call_target="tpu_custom_call" | custom-call | tf_op jit(solution)/shard_map/pallas_call | solution.py:238
  103.7 9.9 %collective-permute-start.21 = (bf16[512,2304]{1,0:T(8,128)(2,1)S(1)}, bf16[512,2304]{1,0:T(8,128)(2,1)S(1)}, u32[]{:S(2)}, u32[]{:S(2)}) collective-permute-start(bf16[512,2304]{1,0:T(8,128)(2,1)S(1)} %get-tuple-element.33), channel_id=1, source_target_pairs={{0,16},{16,0},{1,17},{17,1},{2,18},{18,2},{3,19},{19,3},{4,20},{20... | collective-permute-start | bytes 7077896 | tf_op jit(solution)/shard_map/ppermute | solution.py:369
  113.7 3.6 %shard_map.59.refs_0_ = bf16[512,2304]{1,0:T(8,128)(2,1)S(1)} custom-call(s32[2]{0:T(128)S(1)} %pad_add_fusion.info, bf16[4,512,256]{2,1,0:T(8,128)(2,1)S(1)} %get-tuple-element.30.refs_0_, bf16[1024,2304]{1,0:T(8,128)(2,1)S(1)} %get-tuple-element.31.refs_1_, f32[512,2304]{1,0:T(8,128)S(1)} %get-tuple-element.32.refs_2_), custom_call_target="tpu_custom_call" | custom-call | tf_op jit(solution)/shard_map/pallas_call | solution.py:238
  117.8 1.6 %shard_map.60 = bf16[512,2304]{1,0:T(8,128)(2,1)} custom-call(bf16[512,2304]{1,0:T(8,128)(2,1)S(1)} %shard_map.59.refs_0_, bf16[512,2304]{1,0:T(8,128)(2,1)S(1)} %collective-permute-done.21.refs_1_), custom_call_target="tpu_custom_call" | custom-call | tf_op jit(solution)/shard_map/pallas_call | solution.py:279
  (53 shorter events, 6.6 us)
Async XLA Ops:
  1.8 7.5 %copy-start.2 = (s32[8192]{0:T(1024)S(1)}, s32[8192]{0:T(1024)}, u32[]{:S(2)}) copy-start(s32[8192]{0:T(1024)} %param.10) | copy-start | bytes 98308
  1.9 12.9 %collective-permute-start.12 = (bf16[512,256]{1,0:T(8,128)(2,1)S(1)}, bf16[512,256]{1,0:T(8,128)(2,1)S(1)}, u32[]{:S(2)}, u32[]{:S(2)}) collective-permute-start(bf16[512,256]{1,0:T(8,128)(2,1)S(1)} %pad_maximum_fusion.7), channel_id=1, source_target_pairs={{0,2},{1,3},{2,0},{3,1},{4,6},{5,7},{6,4},{7,5},{8,10},{9,11},{10,... | collective-permute-start | bytes 786440 | tf_op jit(solution)/shard_map/ppermute | solution.py:309
  3.9 13.1 %collective-permute-start.13 = (bf16[512,256]{1,0:T(8,128)(2,1)}, bf16[512,256]{1,0:T(8,128)(2,1)S(1)}, u32[]{:S(2)}, u32[]{:S(2)}) collective-permute-start(bf16[512,256]{1,0:T(8,128)(2,1)} %pad_maximum_fusion.8), channel_id=1, source_target_pairs={{0,3},{1,2},{2,1},{3,0},{4,7},{5,6},{6,5},{7,4},{8,11},{9,10},{10,... | collective-permute-start | bytes 786440 | tf_op jit(solution)/shard_map/ppermute | solution.py:309
  5.1 19.4 %collective-permute-start.1 = (bf16[512,256]{1,0:T(8,128)(2,1)S(1)}, bf16[512,256]{1,0:T(8,128)(2,1)S(1)}, u32[]{:S(2)}, u32[]{:S(2)}) collective-permute-start(bf16[512,256]{1,0:T(8,128)(2,1)S(1)} %pad_maximum_fusion.3), channel_id=1, source_target_pairs={{0,1},{1,0},{2,3},{3,2},{4,5},{5,4},{6,7},{7,6},{8,9},{9,8},{10,11... | collective-permute-start | bytes 786440 | tf_op jit(solution)/shard_map/ppermute | solution.py:309
  6.1 21.5 %collective-permute-start.2 = (bf16[512,256]{1,0:T(8,128)(2,1)}, bf16[512,256]{1,0:T(8,128)(2,1)S(1)}, u32[]{:S(2)}, u32[]{:S(2)}) collective-permute-start(bf16[512,256]{1,0:T(8,128)(2,1)} %pad_maximum_fusion.4), channel_id=1, source_target_pairs={{0,2},{1,3},{2,0},{3,1},{4,6},{5,7},{6,4},{7,5},{8,10},{9,11},{10,... | collective-permute-start | bytes 786440 | tf_op jit(solution)/shard_map/ppermute | solution.py:309
  8.1 14.2 %collective-permute-start.11 = (bf16[512,256]{1,0:T(8,128)(2,1)}, bf16[512,256]{1,0:T(8,128)(2,1)S(1)}, u32[]{:S(2)}, u32[]{:S(2)}) collective-permute-start(bf16[512,256]{1,0:T(8,128)(2,1)} %pad_maximum_fusion.6), channel_id=1, source_target_pairs={{0,1},{1,0},{2,3},{3,2},{4,5},{5,4},{6,7},{7,6},{8,9},{9,8},{10,11... | collective-permute-start | bytes 786440 | tf_op jit(solution)/shard_map/ppermute | solution.py:309
  14.7 16.1 %collective-permute-start.3 = (bf16[512,256]{1,0:T(8,128)(2,1)S(1)}, bf16[512,256]{1,0:T(8,128)(2,1)S(1)}, u32[]{:S(2)}, u32[]{:S(2)}) collective-permute-start(bf16[512,256]{1,0:T(8,128)(2,1)S(1)} %pad_maximum_fusion.5), channel_id=1, source_target_pairs={{0,3},{1,2},{2,1},{3,0},{4,7},{5,6},{6,5},{7,4},{8,11},{9,10},{10,... | collective-permute-start | bytes 786440 | tf_op jit(solution)/shard_map/ppermute | solution.py:309
  17.0 17.5 %collective-permute-start.17 = (bf16[512,256]{1,0:T(8,128)(2,1)S(1)}, bf16[512,256]{1,0:T(8,128)(2,1)S(1)}, u32[]{:S(2)}, u32[]{:S(2)}) collective-permute-start(bf16[512,256]{1,0:T(8,128)(2,1)S(1)} %get-tuple-element.36), channel_id=1, source_target_pairs={{0,3},{1,2},{2,1},{3,0},{4,7},{5,6},{6,5},{7,4},{8,11},{9,10},{10,... | collective-permute-start | bytes 786440 | tf_op jit(solution)/shard_map/ppermute | solution.py:309
  22.3 17.0 %collective-permute-start.15 = (bf16[512,256]{1,0:T(8,128)(2,1)}, bf16[512,256]{1,0:T(8,128)(2,1)}, u32[]{:S(2)}, u32[]{:S(2)}) collective-permute-start(bf16[512,256]{1,0:T(8,128)(2,1)} %get-tuple-element.37), channel_id=1, source_target_pairs={{0,1},{1,0},{2,3},{3,2},{4,5},{5,4},{6,7},{7,6},{8,9},{9,8},{10,11... | collective-permute-start | bytes 786440 | tf_op jit(solution)/shard_map/ppermute | solution.py:309
  24.4 17.2 %collective-permute-start = (bf16[512,512]{1,0:T(8,128)(2,1)S(1)}, bf16[512,512]{1,0:T(8,128)(2,1)S(1)}, u32[]{:S(2)}, u32[]{:S(2)}) collective-permute-start(bf16[512,512]{1,0:T(8,128)(2,1)S(1)} %pad_maximum_fusion.2.refs_5_), channel_id=1, source_target_pairs={{0,4},{1,5},{2,6},{3,7},{4,8},{5,9},{6,10},{7,11},{8,12},{9,13},{1... | collective-permute-start | bytes 1572872 | tf_op jit(solution)/shard_map/ppermute | solution.py:313
  27.7 25.7 %collective-permute-start.14 = (bf16[1536,256]{1,0:T(8,128)(2,1)}, bf16[1536,256]{1,0:T(8,128)(2,1)}, u32[]{:S(2)}, u32[]{:S(2)}) collective-permute-start(bf16[1536,256]{1,0:T(8,128)(2,1)} %pad_maximum_fusion.1), channel_id=1, source_target_pairs={{0,4},{1,5},{2,6},{3,7},{4,8},{5,9},{6,10},{7,11},{8,12},{9,13},{1... | collective-permute-start | bytes 2359304 | tf_op jit(solution)/shard_map/ppermute | solution.py:313
  31.8 40.9 %collective-permute-start.4 = (bf16[1536,256]{1,0:T(8,128)(2,1)}, bf16[1536,256]{1,0:T(8,128)(2,1)}, u32[]{:S(2)}, u32[]{:S(2)}) collective-permute-start(bf16[1536,256]{1,0:T(8,128)(2,1)} %pad_maximum_fusion), channel_id=1, source_target_pairs={{0,4},{1,5},{2,6},{3,7},{4,8},{5,9},{6,10},{7,11},{8,12},{9,13},{1... | collective-permute-start | bytes 2359304 | tf_op jit(solution)/shard_map/ppermute | solution.py:313
  34.5 19.2 %copy-start = (bf16[512,256]{1,0:T(8,128)(2,1)}, bf16[512,256]{1,0:T(8,128)(2,1)S(1)}, u32[]{:S(2)}) copy-start(bf16[512,256]{1,0:T(8,128)(2,1)S(1)} %collective-permute-done.17.refs_12_) | copy-start | bytes 786436
  34.5 6.9 %collective-permute-start.16 = (bf16[512,256]{1,0:T(8,128)(2,1)}, bf16[512,256]{1,0:T(8,128)(2,1)}, u32[]{:S(2)}, u32[]{:S(2)}) collective-permute-start(bf16[512,256]{1,0:T(8,128)(2,1)} %get-tuple-element.43), channel_id=1, source_target_pairs={{0,2},{1,3},{2,0},{3,1},{4,6},{5,7},{6,4},{7,5},{8,10},{9,11},{10,... | collective-permute-start | bytes 786440 | tf_op jit(solution)/shard_map/ppermute | solution.py:309
  39.3 31.1 %collective-permute-start.7 = (bf16[512,256]{1,0:T(8,128)(2,1)}, bf16[512,256]{1,0:T(8,128)(2,1)}, u32[]{:S(2)}, u32[]{:S(2)}) collective-permute-start(bf16[512,256]{1,0:T(8,128)(2,1)} %get-tuple-element.39), channel_id=1, source_target_pairs={{0,3},{1,2},{2,1},{3,0},{4,7},{5,6},{6,5},{7,4},{8,11},{9,10},{10,... | collective-permute-start | bytes 786440 | tf_op jit(solution)/shard_map/ppermute | solution.py:309
  41.4 30.2 %collective-permute-start.6 = (bf16[512,256]{1,0:T(8,128)(2,1)}, bf16[512,256]{1,0:T(8,128)(2,1)}, u32[]{:S(2)}, u32[]{:S(2)}) collective-permute-start(bf16[512,256]{1,0:T(8,128)(2,1)} %get-tuple-element.40), channel_id=1, source_target_pairs={{0,2},{1,3},{2,0},{3,1},{4,6},{5,7},{6,4},{7,5},{8,10},{9,11},{10,... | collective-permute-start | bytes 786440 | tf_op jit(solution)/shard_map/ppermute | solution.py:309
  41.7 31.1 %collective-permute-start.5 = (bf16[512,256]{1,0:T(8,128)(2,1)}, bf16[512,256]{1,0:T(8,128)(2,1)}, u32[]{:S(2)}, u32[]{:S(2)}) collective-permute-start(bf16[512,256]{1,0:T(8,128)(2,1)} %get-tuple-element.41), channel_id=1, source_target_pairs={{0,1},{1,0},{2,3},{3,2},{4,5},{5,4},{6,7},{7,6},{8,9},{9,8},{10,11... | collective-permute-start | bytes 786440 | tf_op jit(solution)/shard_map/ppermute | solution.py:309
  53.7 1.0 copy-start.1
  70.1 19.8 %collective-permute-start.18 = (bf16[512,256]{1,0:T(8,128)(2,1)S(1)}, bf16[512,256]{1,0:T(8,128)(2,1)S(1)}, u32[]{:S(2)}, u32[]{:S(2)}) collective-permute-start(bf16[512,256]{1,0:T(8,128)(2,1)S(1)} %get-tuple-element.25), channel_id=1, source_target_pairs={{0,1},{1,0},{2,3},{3,2},{4,5},{5,4},{6,7},{7,6},{8,9},{9,8},{10,11... | collective-permute-start | bytes 786440 | tf_op jit(solution)/shard_map/ppermute | solution.py:309
  70.3 20.8 %collective-permute-start.19 = (bf16[512,256]{1,0:T(8,128)(2,1)}, bf16[512,256]{1,0:T(8,128)(2,1)S(1)}, u32[]{:S(2)}, u32[]{:S(2)}) collective-permute-start(bf16[512,256]{1,0:T(8,128)(2,1)} %get-tuple-element.26), channel_id=1, source_target_pairs={{0,2},{1,3},{2,0},{3,1},{4,6},{5,7},{6,4},{7,5},{8,10},{9,11},{10,... | collective-permute-start | bytes 786440 | tf_op jit(solution)/shard_map/ppermute | solution.py:309
  71.6 19.6 %collective-permute-start.20 = (bf16[512,256]{1,0:T(8,128)(2,1)}, bf16[512,256]{1,0:T(8,128)(2,1)S(1)}, u32[]{:S(2)}, u32[]{:S(2)}) collective-permute-start(bf16[512,256]{1,0:T(8,128)(2,1)} %get-tuple-element.27), channel_id=1, source_target_pairs={{0,3},{1,2},{2,1},{3,0},{4,7},{5,6},{6,5},{7,4},{8,11},{9,10},{10,... | collective-permute-start | bytes 786440 | tf_op jit(solution)/shard_map/ppermute | solution.py:309
  88.4 11.7 %collective-permute-start.8 = (bf16[512,256]{1,0:T(8,128)(2,1)}, bf16[512,256]{1,0:T(8,128)(2,1)S(1)}, u32[]{:S(2)}, u32[]{:S(2)}) collective-permute-start(bf16[512,256]{1,0:T(8,128)(2,1)} %get-tuple-element.21), channel_id=1, source_target_pairs={{0,1},{1,0},{2,3},{3,2},{4,5},{5,4},{6,7},{7,6},{8,9},{9,8},{10,11... | collective-permute-start | bytes 786440 | tf_op jit(solution)/shard_map/ppermute | solution.py:309
  88.6 11.5 %collective-permute-start.9 = (bf16[512,256]{1,0:T(8,128)(2,1)}, bf16[512,256]{1,0:T(8,128)(2,1)S(1)}, u32[]{:S(2)}, u32[]{:S(2)}) collective-permute-start(bf16[512,256]{1,0:T(8,128)(2,1)} %get-tuple-element.22), channel_id=1, source_target_pairs={{0,2},{1,3},{2,0},{3,1},{4,6},{5,7},{6,4},{7,5},{8,10},{9,11},{10,... | collective-permute-start | bytes 786440 | tf_op jit(solution)/shard_map/ppermute | solution.py:309
  89.8 10.2 %collective-permute-start.10 = (bf16[512,256]{1,0:T(8,128)(2,1)}, bf16[512,256]{1,0:T(8,128)(2,1)S(1)}, u32[]{:S(2)}, u32[]{:S(2)}) collective-permute-start(bf16[512,256]{1,0:T(8,128)(2,1)} %get-tuple-element.23), channel_id=1, source_target_pairs={{0,3},{1,2},{2,1},{3,0},{4,7},{5,6},{6,5},{7,4},{8,11},{9,10},{10,... | collective-permute-start | bytes 786440 | tf_op jit(solution)/shard_map/ppermute | solution.py:309
  103.7 14.0 %collective-permute-start.21 = (bf16[512,2304]{1,0:T(8,128)(2,1)S(1)}, bf16[512,2304]{1,0:T(8,128)(2,1)S(1)}, u32[]{:S(2)}, u32[]{:S(2)}) collective-permute-start(bf16[512,2304]{1,0:T(8,128)(2,1)S(1)} %get-tuple-element.33), channel_id=1, source_target_pairs={{0,16},{16,0},{1,17},{17,1},{2,18},{18,2},{3,19},{19,3},{4,20},{20... | collective-permute-start | bytes 7077896 | tf_op jit(solution)/shard_map/ppermute | solution.py:369

commit v2 on v1

--- a/solution.py
+++ b/solution.py
@@ -46,10 +46,20 @@
         v_all[slot, :, :HEAD_DIM] = ref[at, column + HEAD_DIM : column + 2 * HEAD_DIM]
 
     own_column = chunk * 2 * HEAD_DIM
+    earliest = meta[1 + start]
+    for n in range(1, count):
+        earliest = jnp.minimum(earliest, meta[1 + start + stride * n])
     for p in range(before):
-        place(far[2 * p], 0, own_column, p * group + me)
-        for r in range(1, group):
-            place(far[2 * p + 1], (r - 1) * rows, 0, p * group + (me ^ r))
+        for r in range(group):
+            slot = p * group + (me ^ r)
+
+            @pl.when(slot >= earliest)
+            def _():
+                if r == 0:
+                    place(far[2 * p], 0, own_column, slot)
+                else:
+                    place(far[2 * p + 1], (r - 1) * rows, 0, slot)
+
     for r in range(group):
         place(near[r], 0, 0 if r else own_column, base + (me ^ r))
     for n in range(count):
@@ -134,7 +144,15 @@
                 acc[h] += weighted(j, h, 0, rows, rows)
             return c
 
-        lax.fori_loop(first, at, mix_step, 0)
+        def mix_two(n, c):
+            j = first + 2 * n
+            for h in range(ratio):
+                acc[h] += weighted(j, h, 0, rows, rows) + weighted(j + 1, h, 0, rows, rows)
+            return c
+
+        pairs = lax.shift_right_logical(at - first, 1)
+        lax.fori_loop(0, pairs, mix_two, 0)
+        lax.fori_loop(first + 2 * pairs, at, mix_step, 0)
         for h in range(ratio):
             o = (acc[h, :, :HEAD_DIM] / acc[h, :, HEAD_DIM:]).astype(jnp.bfloat16)
             for k in range(count):
@@ -320,12 +338,13 @@
         return [columns_of(keys, at, 1), columns_of(values, at, 1)]
 
     own = jnp.concatenate([piece for c in range(chunks) for piece in pair_of(c, 0)], axis=1)
-    near = [[own] + [swap(jnp.concatenate(pair_of(c, r), axis=1), r) for r in range(1, group)] for c in range(chunks)]
+    pieces = [[jnp.concatenate(pair_of(c, r), axis=1) for r in range(1, group)] for c in range(chunks)]
+    near = [[own] + [swap(piece, r + 1) for r, piece in enumerate(pieces[c])] for c in range(chunks)]
     far_own = [upward(own, p) for p in range(before, 0, -1)]
     own_q = [[swap(columns_of(queries, c * group + (me ^ r), ratio), r) for r in range(group)] for c in range(chunks)]
     far = []
     for c in range(chunks):
-        rest = jnp.concatenate(near[c][1:], axis=0)
+        rest = jnp.concatenate(near[c][1:], axis=0) if group > 1 else own
         moved = [upward(rest, p) for p in range(before, 0, -1)]
         far.append([piece for pair in zip(far_own, moved) for piece in pair])
 

time: 120 us -> 118 us (0.983)
  Pallas kernels: 48.7 us -> 47.3 us
    pallas_call x2, Pallas kernels: 31 us -> 29.6 us  [attend(): pl.pallas_call(lambda *refs: attend_kernel(chunk, group, before, ratio, r...]
where the time goes in v2:
time: 118 us
  Pallas kernels  47.3 us (40%)
  starting transfers between devices  35.8 us (30%)
  waiting for transfers between devices  22.6 us (19%)
  local copies, waits for them, and re-layouts  7.21 us (6%)
  other arithmetic  4.76 us (4%)
    pallas_call x2, Pallas kernels, attend(): pl.pallas_call(lambda *refs: attend_kernel(chunk, group, before, ratio, r...  29.6 us
    ppermute x18, starting transfers between devices, swap(): return lax.ppermute(value, 'seq', [(s, s ^ r) for s in range(seq_size)])  17.6 us
    pallas_call x3, Pallas kernels, project(): pl.pallas_call(kernel, out_shape=shapes, in_specs=[pl.BlockSpec(memory_sp...  16.1 us
    ppermute x3, waiting for transfers between devices, upward(): lax.ppermute(value, 'seq', [(s, s + step) for s in range(seq_size - step)])  11.4 us
    ppermute x18, waiting for transfers between devices, swap(): return lax.ppermute(value, 'seq', [(s, s ^ r) for s in range(seq_size)])  10.7 us
    ppermute x1, starting transfers between devices, body(): sent[d - 1] = lax.ppermute(sent[d - 1], 'head', ring)  9.87 us
    ppermute x3, starting transfers between devices, upward(): lax.ppermute(value, 'seq', [(s, s + step) for s in range(seq_size - step)])  8.31 us
    dynamic_slice x2, local copies, waits for them, and re-layouts, columns_of(): lax.dynamic_slice_in_dim(value, at * heads * HEAD_DIM, heads * HEAD_DIM, 1)  4.44 us
  transfers between devices with their start and end apart: 22, of which 6 were waited for; matrix products, arithmetic and copies ran while one was open for 8% of the time, Pallas kernels for 36%

profile of v2, /device:TPU:9, one launch (start us, length us, event | category | flops | bytes accessed | tf_op | source)
XLA Modules:
  0.0 118.1 jit_solution(5858467570217311663)
XLA Ops:
  0.0 1.8 %constant_dynamic-slice_fusion.8 = (bf16[512,128]{1,0:T(8,128)(2,1)S(1)}, bf16[512,128]{1,0:T(8,128)(2,1)S(1)}, bf16[512,128]{1,0:T(8,128)(2,1)S(1)}, bf16[512,1...) fusion(bf16[512,1024]{1,0:T(8,128)(2,1)} %param.9, ...), kind=kLoop, calls=%fused_computation.21 | loop fusion | bytes 4194336 | tf_op jit(solution)/shard_map/dynamic_slice | solution.py:334
  1.9 1.3 %collective-permute-start.12 = (bf16[512,256]{1,0:T(8,128)(2,1)S(1)}, bf16[512,256]{1,0:T(8,128)(2,1)S(1)}, u32[]{:S(2)}, u32[]{:S(2)}) collective-permute-start(bf16[512,256]{1,0:T(8,128)(2,1)S(1)} %pad_maximum_fusion.7), channel_id=1, source_target_pairs={{0,2},{1,3},{2,0},{3,1},{4,6},{5,7},{6,4},{7,5},{8,10},{9,11},{10,... | collective-permute-start | bytes 786440 | tf_op jit(solution)/shard_map/ppermute | solution.py:327
  3.9 1.2 collective-permute-start.13
  5.4 0.7 pad_maximum_fusion.4
  6.1 1.2 %collective-permute-start.2 = (bf16[512,256]{1,0:T(8,128)(2,1)}, bf16[512,256]{1,0:T(8,128)(2,1)S(1)}, u32[]{:S(2)}, u32[]{:S(2)}) collective-permute-start(bf16[512,256]{1,0:T(8,128)(2,1)} %pad_maximum_fusion.4), channel_id=1, source_target_pairs={{0,2},{1,3},{2,0},{3,1},{4,6},{5,7},{6,4},{7,5},{8,10},{9,11},{10,... | collective-permute-start | bytes 786440 | tf_op jit(solution)/shard_map/ppermute | solution.py:327
  8.1 1.2 %collective-permute-start.11 = (bf16[512,256]{1,0:T(8,128)(2,1)}, bf16[512,256]{1,0:T(8,128)(2,1)S(1)}, u32[]{:S(2)}, u32[]{:S(2)}) collective-permute-start(bf16[512,256]{1,0:T(8,128)(2,1)} %pad_maximum_fusion.6), channel_id=1, source_target_pairs={{0,1},{1,0},{2,3},{3,2},{4,5},{5,4},{6,7},{7,6},{8,9},{9,8},{10,11... | collective-permute-start | bytes 786440 | tf_op jit(solution)/shard_map/ppermute | solution.py:327
  10.9 2.6 %constant_dynamic-slice_fusion = (bf16[512,256]{1,0:T(8,128)(2,1)S(1)}, bf16[512,256]{1,0:T(8,128)(2,1)}, bf16[512,256]{1,0:T(8,128)(2,1)S(1)}, bf16[512,256]{1,...) fusion(bf16[512,2048]{1,0:T(8,128)(2,1)} %param.7, ...), kind=kLoop, calls=%fused_computation.13 | loop fusion | bytes 4194336 | tf_op jit(solution)/shard_map/dynamic_slice | solution.py:334
  13.6 1.2 collective-permute-done.12.refs_7_
  14.7 2.2 %collective-permute-start.3 = (bf16[512,256]{1,0:T(8,128)(2,1)S(1)}, bf16[512,256]{1,0:T(8,128)(2,1)S(1)}, u32[]{:S(2)}, u32[]{:S(2)}) collective-permute-start(bf16[512,256]{1,0:T(8,128)(2,1)S(1)} %pad_maximum_fusion.5), channel_id=1, source_target_pairs={{0,3},{1,2},{2,1},{3,0},{4,7},{5,6},{6,5},{7,4},{8,11},{9,10},{10,... | collective-permute-start | bytes 786440 | tf_op jit(solution)/shard_map/ppermute | solution.py:327
  17.2 5.1 %collective-permute-done.11.refs_6_ = bf16[512,256]{1,0:T(8,128)(2,1)S(1)} collective-permute-done((bf16[512,256]{1,0:T(8,128)(2,1)}, bf16[512,256]{1,0:T(8,128)(2,1)S(1)}, u32[]{:S(2)}, u32[]{:S(2)}) %collective-permute-start.11) | collective-permute-done | bytes 262176 | tf_op jit(solution)/shard_map/ppermute | solution.py:327
  22.3 1.2 %collective-permute-start.15 = (bf16[512,256]{1,0:T(8,128)(2,1)}, bf16[512,256]{1,0:T(8,128)(2,1)}, u32[]{:S(2)}, u32[]{:S(2)}) collective-permute-start(bf16[512,256]{1,0:T(8,128)(2,1)} %get-tuple-element.37), channel_id=1, source_target_pairs={{0,1},{1,0},{2,3},{3,2},{4,5},{5,4},{6,7},{7,6},{8,9},{9,8},{10,11... | collective-permute-start | bytes 786440 | tf_op jit(solution)/shard_map/ppermute | solution.py:327
  23.5 0.9 pad_maximum_fusion.1
  24.4 3.2 %collective-permute-start = (bf16[512,512]{1,0:T(8,128)(2,1)S(1)}, bf16[512,512]{1,0:T(8,128)(2,1)S(1)}, u32[]{:S(2)}, u32[]{:S(2)}) collective-permute-start(bf16[512,512]{1,0:T(8,128)(2,1)S(1)} %pad_maximum_fusion.2.refs_5_), channel_id=1, source_target_pairs={{0,4},{1,5},{2,6},{3,7},{4,8},{5,9},{6,10},{7,11},{8,12},{9,13},{1... | collective-permute-start | bytes 1572872 | tf_op jit(solution)/shard_map/ppermute | solution.py:331
  27.7 3.2 %collective-permute-start.14 = (bf16[1536,256]{1,0:T(8,128)(2,1)}, bf16[1536,256]{1,0:T(8,128)(2,1)}, u32[]{:S(2)}, u32[]{:S(2)}) collective-permute-start(bf16[1536,256]{1,0:T(8,128)(2,1)} %pad_maximum_fusion.1), channel_id=1, source_target_pairs={{0,4},{1,5},{2,6},{3,7},{4,8},{5,9},{6,10},{7,11},{8,12},{9,13},{1... | collective-permute-start | bytes 2359304 | tf_op jit(solution)/shard_map/ppermute | solution.py:331
  30.9 0.9 pad_maximum_fusion
  31.8 1.9 %collective-permute-start.4 = (bf16[1536,256]{1,0:T(8,128)(2,1)}, bf16[1536,256]{1,0:T(8,128)(2,1)}, u32[]{:S(2)}, u32[]{:S(2)}) collective-permute-start(bf16[1536,256]{1,0:T(8,128)(2,1)} %pad_maximum_fusion), channel_id=1, source_target_pairs={{0,4},{1,5},{2,6},{3,7},{4,8},{5,9},{6,10},{7,11},{8,12},{9,13},{1... | collective-permute-start | bytes 2359304 | tf_op jit(solution)/shard_map/ppermute | solution.py:331
  34.5 0.8 collective-permute-start.16
  35.4 3.9 %collective-permute-done.15.refs_10_ = bf16[512,256]{1,0:T(8,128)(2,1)} collective-permute-done((bf16[512,256]{1,0:T(8,128)(2,1)}, bf16[512,256]{1,0:T(8,128)(2,1)}, u32[]{:S(2)}, u32[]{:S(2)}) %collective-permute-start.15) | collective-permute-done | bytes 262176 | tf_op jit(solution)/shard_map/ppermute | solution.py:327
  39.3 2.2 %collective-permute-start.7 = (bf16[512,256]{1,0:T(8,128)(2,1)}, bf16[512,256]{1,0:T(8,128)(2,1)}, u32[]{:S(2)}, u32[]{:S(2)}) collective-permute-start(bf16[512,256]{1,0:T(8,128)(2,1)} %get-tuple-element.39), channel_id=1, source_target_pairs={{0,3},{1,2},{2,1},{3,0},{4,7},{5,6},{6,5},{7,4},{8,11},{9,10},{10,... | collective-permute-start | bytes 786440 | tf_op jit(solution)/shard_map/ppermute | solution.py:327
  41.9 11.4 %collective-permute-done.14.refs_4_ = bf16[1536,256]{1,0:T(8,128)(2,1)} collective-permute-done((bf16[1536,256]{1,0:T(8,128)(2,1)}, bf16[1536,256]{1,0:T(8,128)(2,1)}, u32[]{:S(2)}, u32[]{:S(2)}) %collective-permute-start.14) | collective-permute-done | bytes 786464 | tf_op jit(solution)/shard_map/ppermute | solution.py:331
  53.7 0.9 copy-done.1
  54.7 14.6 %shard_map.56 = (bf16[512,256]{1,0:T(8,128)(2,1)S(1)}, bf16[512,256]{1,0:T(8,128)(2,1)S(1)}, bf16[512,256]{1,0:T(8,128)(2,1)}, bf16[512,256]{1,0:T(8,128)(2,1)}) custom-call(s32[9]{0:T(128)S(1)} %pad_add_fusion.2.refs_0_, s32[4,512,128]{2,1,0:T(8,128)S(1)} %broadcast_in_dim.5.refs_1_, s32[8,1,512]{2,1,0:T(1,128)S(1)} %bitcast.4, ...), custom_call_target="tpu_custom_call" | custom-call | tf_op jit(solution)/shard_map/pallas_call | solution.py:176
  69.5 1.3 %collective-permute-start.19 = (bf16[512,256]{1,0:T(8,128)(2,1)}, bf16[512,256]{1,0:T(8,128)(2,1)S(1)}, u32[]{:S(2)}, u32[]{:S(2)}) collective-permute-start(bf16[512,256]{1,0:T(8,128)(2,1)} %get-tuple-element.26), channel_id=1, source_target_pairs={{0,2},{1,3},{2,0},{3,1},{4,6},{5,7},{6,4},{7,5},{8,10},{9,11},{10,... | collective-permute-start | bytes 786440 | tf_op jit(solution)/shard_map/ppermute | solution.py:327
  70.8 1.1 collective-permute-start.20
  71.9 15.0 %shard_map.55 = (bf16[512,256]{1,0:T(8,128)(2,1)S(1)}, bf16[512,256]{1,0:T(8,128)(2,1)}, bf16[512,256]{1,0:T(8,128)(2,1)}, bf16[512,256]{1,0:T(8,128)(2,1)}) custom-call(s32[9]{0:T(128)S(1)} %pad_add_fusion.2.refs_0_, s32[4,512,128]{2,1,0:T(8,128)S(1)} %broadcast_in_dim.5.refs_1_, s32[8,1,512]{2,1,0:T(1,128)S(1)} %bitcast.5, ...), custom_call_target="tpu_custom_call" | custom-call | tf_op jit(solution)/shard_map/pallas_call | solution.py:176
  87.2 1.3 %collective-permute-start.9 = (bf16[512,256]{1,0:T(8,128)(2,1)}, bf16[512,256]{1,0:T(8,128)(2,1)S(1)}, u32[]{:S(2)}, u32[]{:S(2)}) collective-permute-start(bf16[512,256]{1,0:T(8,128)(2,1)} %get-tuple-element.22), channel_id=1, source_target_pairs={{0,2},{1,3},{2,0},{3,1},{4,6},{5,7},{6,4},{7,5},{8,10},{9,11},{10,... | collective-permute-start | bytes 786440 | tf_op jit(solution)/shard_map/ppermute | solution.py:327
  88.4 1.1 collective-permute-start.10
  89.7 8.9 %shard_map.57 = (f32[512,2304]{1,0:T(8,128)S(1)}, f32[512,2304]{1,0:T(8,128)S(1)}, bf16[4,512,256]{2,1,0:T(8,128)(2,1)}, bf16[1024,2304]{1,0:T(8,128)(2,1)S(1)}, bf16[1024,2304]{1,0:T(8,128)(2,1)S(1)}) custom-call(s32[3]{0:T(128)S(1)} %pad_add_fusion.3.info, bf16[512,256]{1,0:T(8,128)(2,1)S(1)} %get-tuple-element.24.refs_0_, ...), custom_call_target="tpu_custom_call" | custom-call | tf_op jit(solution)/shard_map/pallas_call | solution.py:256
  98.7 3.6 %shard_map.58 = (bf16[512,2304]{1,0:T(8,128)(2,1)S(1)}, bf16[4,512,256]{2,1,0:T(8,128)(2,1)S(1)}) custom-call(s32[2]{0:T(128)S(1)} %pad_add_fusion.1.info, bf16[512,256]{1,0:T(8,128)(2,1)S(1)} %get-tuple-element.20.refs_0_, bf16[512,256]{1,0:T(8,128)(2,1)S(1)} %collective-permute-done.8.refs_1_, bf16[512,256]{1,0:T(8,128)(2,1)S(1)} %collective-permute-done.9.refs_2_, ...), custom_call_target="tpu_custom_call" | custom-call | tf_op jit(solution)/shard_map/pallas_call | solution.py:256
  102.3 9.9 %collective-permute-start.21 = (bf16[512,2304]{1,0:T(8,128)(2,1)S(1)}, bf16[512,2304]{1,0:T(8,128)(2,1)S(1)}, u32[]{:S(2)}, u32[]{:S(2)}) collective-permute-start(bf16[512,2304]{1,0:T(8,128)(2,1)S(1)} %get-tuple-element.33), channel_id=1, source_target_pairs={{0,16},{16,0},{1,17},{17,1},{2,18},{18,2},{3,19},{19,3},{4,20},{20... | collective-permute-start | bytes 7077896 | tf_op jit(solution)/shard_map/ppermute | solution.py:388
  112.3 3.6 %shard_map.59.refs_0_ = bf16[512,2304]{1,0:T(8,128)(2,1)S(1)} custom-call(s32[2]{0:T(128)S(1)} %pad_add_fusion.info, bf16[4,512,256]{2,1,0:T(8,128)(2,1)S(1)} %get-tuple-element.30.refs_0_, bf16[1024,2304]{1,0:T(8,128)(2,1)S(1)} %get-tuple-element.31.refs_1_, f32[512,2304]{1,0:T(8,128)S(1)} %get-tuple-element.32.refs_2_), custom_call_target="tpu_custom_call" | custom-call | tf_op jit(solution)/shard_map/pallas_call | solution.py:256
  116.3 1.6 %shard_map.60 = bf16[512,2304]{1,0:T(8,128)(2,1)} custom-call(bf16[512,2304]{1,0:T(8,128)(2,1)S(1)} %shard_map.59.refs_0_, bf16[512,2304]{1,0:T(8,128)(2,1)S(1)} %collective-permute-done.21.refs_1_), custom_call_target="tpu_custom_call" | custom-call | tf_op jit(solution)/shard_map/pallas_call | solution.py:297
  (53 shorter events, 6.7 us)
Async XLA Ops:
  1.8 7.5 %copy-start.2 = (s32[8192]{0:T(1024)S(1)}, s32[8192]{0:T(1024)}, u32[]{:S(2)}) copy-start(s32[8192]{0:T(1024)} %param.10) | copy-start | bytes 98308
  1.9 12.9 %collective-permute-start.12 = (bf16[512,256]{1,0:T(8,128)(2,1)S(1)}, bf16[512,256]{1,0:T(8,128)(2,1)S(1)}, u32[]{:S(2)}, u32[]{:S(2)}) collective-permute-start(bf16[512,256]{1,0:T(8,128)(2,1)S(1)} %pad_maximum_fusion.7), channel_id=1, source_target_pairs={{0,2},{1,3},{2,0},{3,1},{4,6},{5,7},{6,4},{7,5},{8,10},{9,11},{10,... | collective-permute-start | bytes 786440 | tf_op jit(solution)/shard_map/ppermute | solution.py:327
  3.9 13.1 %collective-permute-start.13 = (bf16[512,256]{1,0:T(8,128)(2,1)}, bf16[512,256]{1,0:T(8,128)(2,1)S(1)}, u32[]{:S(2)}, u32[]{:S(2)}) collective-permute-start(bf16[512,256]{1,0:T(8,128)(2,1)} %pad_maximum_fusion.8), channel_id=1, source_target_pairs={{0,3},{1,2},{2,1},{3,0},{4,7},{5,6},{6,5},{7,4},{8,11},{9,10},{10,... | collective-permute-start | bytes 786440 | tf_op jit(solution)/shard_map/ppermute | solution.py:327
  5.1 19.4 %collective-permute-start.1 = (bf16[512,256]{1,0:T(8,128)(2,1)S(1)}, bf16[512,256]{1,0:T(8,128)(2,1)S(1)}, u32[]{:S(2)}, u32[]{:S(2)}) collective-permute-start(bf16[512,256]{1,0:T(8,128)(2,1)S(1)} %pad_maximum_fusion.3), channel_id=1, source_target_pairs={{0,1},{1,0},{2,3},{3,2},{4,5},{5,4},{6,7},{7,6},{8,9},{9,8},{10,11... | collective-permute-start | bytes 786440 | tf_op jit(solution)/shard_map/ppermute | solution.py:327
  6.1 21.5 %collective-permute-start.2 = (bf16[512,256]{1,0:T(8,128)(2,1)}, bf16[512,256]{1,0:T(8,128)(2,1)S(1)}, u32[]{:S(2)}, u32[]{:S(2)}) collective-permute-start(bf16[512,256]{1,0:T(8,128)(2,1)} %pad_maximum_fusion.4), channel_id=1, source_target_pairs={{0,2},{1,3},{2,0},{3,1},{4,6},{5,7},{6,4},{7,5},{8,10},{9,11},{10,... | collective-permute-start | bytes 786440 | tf_op jit(solution)/shard_map/ppermute | solution.py:327
  8.1 14.2 %collective-permute-start.11 = (bf16[512,256]{1,0:T(8,128)(2,1)}, bf16[512,256]{1,0:T(8,128)(2,1)S(1)}, u32[]{:S(2)}, u32[]{:S(2)}) collective-permute-start(bf16[512,256]{1,0:T(8,128)(2,1)} %pad_maximum_fusion.6), channel_id=1, source_target_pairs={{0,1},{1,0},{2,3},{3,2},{4,5},{5,4},{6,7},{7,6},{8,9},{9,8},{10,11... | collective-permute-start | bytes 786440 | tf_op jit(solution)/shard_map/ppermute | solution.py:327
  14.7 16.1 %collective-permute-start.3 = (bf16[512,256]{1,0:T(8,128)(2,1)S(1)}, bf16[512,256]{1,0:T(8,128)(2,1)S(1)}, u32[]{:S(2)}, u32[]{:S(2)}) collective-permute-start(bf16[512,256]{1,0:T(8,128)(2,1)S(1)} %pad_maximum_fusion.5), channel_id=1, source_target_pairs={{0,3},{1,2},{2,1},{3,0},{4,7},{5,6},{6,5},{7,4},{8,11},{9,10},{10,... | collective-permute-start | bytes 786440 | tf_op jit(solution)/shard_map/ppermute | solution.py:327
  17.0 17.5 %collective-permute-start.17 = (bf16[512,256]{1,0:T(8,128)(2,1)S(1)}, bf16[512,256]{1,0:T(8,128)(2,1)S(1)}, u32[]{:S(2)}, u32[]{:S(2)}) collective-permute-start(bf16[512,256]{1,0:T(8,128)(2,1)S(1)} %get-tuple-element.36), channel_id=1, source_target_pairs={{0,3},{1,2},{2,1},{3,0},{4,7},{5,6},{6,5},{7,4},{8,11},{9,10},{10,... | collective-permute-start | bytes 786440 | tf_op jit(solution)/shard_map/ppermute | solution.py:327
  22.3 17.0 %collective-permute-start.15 = (bf16[512,256]{1,0:T(8,128)(2,1)}, bf16[512,256]{1,0:T(8,128)(2,1)}, u32[]{:S(2)}, u32[]{:S(2)}) collective-permute-start(bf16[512,256]{1,0:T(8,128)(2,1)} %get-tuple-element.37), channel_id=1, source_target_pairs={{0,1},{1,0},{2,3},{3,2},{4,5},{5,4},{6,7},{7,6},{8,9},{9,8},{10,11... | collective-permute-start | bytes 786440 | tf_op jit(solution)/shard_map/ppermute | solution.py:327
  24.4 17.2 %collective-permute-start = (bf16[512,512]{1,0:T(8,128)(2,1)S(1)}, bf16[512,512]{1,0:T(8,128)(2,1)S(1)}, u32[]{:S(2)}, u32[]{:S(2)}) collective-permute-start(bf16[512,512]{1,0:T(8,128)(2,1)S(1)} %pad_maximum_fusion.2.refs_5_), channel_id=1, source_target_pairs={{0,4},{1,5},{2,6},{3,7},{4,8},{5,9},{6,10},{7,11},{8,12},{9,13},{1... | collective-permute-start | bytes 1572872 | tf_op jit(solution)/shard_map/ppermute | solution.py:331
  27.7 25.7 %collective-permute-start.14 = (bf16[1536,256]{1,0:T(8,128)(2,1)}, bf16[1536,256]{1,0:T(8,128)(2,1)}, u32[]{:S(2)}, u32[]{:S(2)}) collective-permute-start(bf16[1536,256]{1,0:T(8,128)(2,1)} %pad_maximum_fusion.1), channel_id=1, source_target_pairs={{0,4},{1,5},{2,6},{3,7},{4,8},{5,9},{6,10},{7,11},{8,12},{9,13},{1... | collective-permute-start | bytes 2359304 | tf_op jit(solution)/shard_map/ppermute | solution.py:331
  31.8 40.1 %collective-permute-start.4 = (bf16[1536,256]{1,0:T(8,128)(2,1)}, bf16[1536,256]{1,0:T(8,128)(2,1)}, u32[]{:S(2)}, u32[]{:S(2)}) collective-permute-start(bf16[1536,256]{1,0:T(8,128)(2,1)} %pad_maximum_fusion), channel_id=1, source_target_pairs={{0,4},{1,5},{2,6},{3,7},{4,8},{5,9},{6,10},{7,11},{8,12},{9,13},{1... | collective-permute-start | bytes 2359304 | tf_op jit(solution)/shard_map/ppermute | solution.py:331
  34.5 19.2 %copy-start = (bf16[512,256]{1,0:T(8,128)(2,1)}, bf16[512,256]{1,0:T(8,128)(2,1)S(1)}, u32[]{:S(2)}) copy-start(bf16[512,256]{1,0:T(8,128)(2,1)S(1)} %collective-permute-done.17.refs_12_) | copy-start | bytes 786436
  34.5 6.9 %collective-permute-start.16 = (bf16[512,256]{1,0:T(8,128)(2,1)}, bf16[512,256]{1,0:T(8,128)(2,1)}, u32[]{:S(2)}, u32[]{:S(2)}) collective-permute-start(bf16[512,256]{1,0:T(8,128)(2,1)} %get-tuple-element.43), channel_id=1, source_target_pairs={{0,2},{1,3},{2,0},{3,1},{4,6},{5,7},{6,4},{7,5},{8,10},{9,11},{10,... | collective-permute-start | bytes 786440 | tf_op jit(solution)/shard_map/ppermute | solution.py:327
  39.3 30.3 %collective-permute-start.7 = (bf16[512,256]{1,0:T(8,128)(2,1)}, bf16[512,256]{1,0:T(8,128)(2,1)}, u32[]{:S(2)}, u32[]{:S(2)}) collective-permute-start(bf16[512,256]{1,0:T(8,128)(2,1)} %get-tuple-element.39), channel_id=1, source_target_pairs={{0,3},{1,2},{2,1},{3,0},{4,7},{5,6},{6,5},{7,4},{8,11},{9,10},{10,... | collective-permute-start | bytes 786440 | tf_op jit(solution)/shard_map/ppermute | solution.py:327
  41.4 29.4 %collective-permute-start.6 = (bf16[512,256]{1,0:T(8,128)(2,1)}, bf16[512,256]{1,0:T(8,128)(2,1)}, u32[]{:S(2)}, u32[]{:S(2)}) collective-permute-start(bf16[512,256]{1,0:T(8,128)(2,1)} %get-tuple-element.40), channel_id=1, source_target_pairs={{0,2},{1,3},{2,0},{3,1},{4,6},{5,7},{6,4},{7,5},{8,10},{9,11},{10,... | collective-permute-start | bytes 786440 | tf_op jit(solution)/shard_map/ppermute | solution.py:327
  41.7 30.3 %collective-permute-start.5 = (bf16[512,256]{1,0:T(8,128)(2,1)}, bf16[512,256]{1,0:T(8,128)(2,1)}, u32[]{:S(2)}, u32[]{:S(2)}) collective-permute-start(bf16[512,256]{1,0:T(8,128)(2,1)} %get-tuple-element.41), channel_id=1, source_target_pairs={{0,1},{1,0},{2,3},{3,2},{4,5},{5,4},{6,7},{7,6},{8,9},{9,8},{10,11... | collective-permute-start | bytes 786440 | tf_op jit(solution)/shard_map/ppermute | solution.py:327
  53.7 1.0 copy-start.1
  69.3 19.2 %collective-permute-start.18 = (bf16[512,256]{1,0:T(8,128)(2,1)S(1)}, bf16[512,256]{1,0:T(8,128)(2,1)S(1)}, u32[]{:S(2)}, u32[]{:S(2)}) collective-permute-start(bf16[512,256]{1,0:T(8,128)(2,1)S(1)} %get-tuple-element.25), channel_id=1, source_target_pairs={{0,1},{1,0},{2,3},{3,2},{4,5},{5,4},{6,7},{7,6},{8,9},{9,8},{10,11... | collective-permute-start | bytes 786440 | tf_op jit(solution)/shard_map/ppermute | solution.py:327
  69.5 20.2 %collective-permute-start.19 = (bf16[512,256]{1,0:T(8,128)(2,1)}, bf16[512,256]{1,0:T(8,128)(2,1)S(1)}, u32[]{:S(2)}, u32[]{:S(2)}) collective-permute-start(bf16[512,256]{1,0:T(8,128)(2,1)} %get-tuple-element.26), channel_id=1, source_target_pairs={{0,2},{1,3},{2,0},{3,1},{4,6},{5,7},{6,4},{7,5},{8,10},{9,11},{10,... | collective-permute-start | bytes 786440 | tf_op jit(solution)/shard_map/ppermute | solution.py:327
  70.8 18.9 %collective-permute-start.20 = (bf16[512,256]{1,0:T(8,128)(2,1)}, bf16[512,256]{1,0:T(8,128)(2,1)S(1)}, u32[]{:S(2)}, u32[]{:S(2)}) collective-permute-start(bf16[512,256]{1,0:T(8,128)(2,1)} %get-tuple-element.27), channel_id=1, source_target_pairs={{0,3},{1,2},{2,1},{3,0},{4,7},{5,6},{6,5},{7,4},{8,11},{9,10},{10,... | collective-permute-start | bytes 786440 | tf_op jit(solution)/shard_map/ppermute | solution.py:327
  86.9 11.7 %collective-permute-start.8 = (bf16[512,256]{1,0:T(8,128)(2,1)}, bf16[512,256]{1,0:T(8,128)(2,1)S(1)}, u32[]{:S(2)}, u32[]{:S(2)}) collective-permute-start(bf16[512,256]{1,0:T(8,128)(2,1)} %get-tuple-element.21), channel_id=1, source_target_pairs={{0,1},{1,0},{2,3},{3,2},{4,5},{5,4},{6,7},{7,6},{8,9},{9,8},{10,11... | collective-permute-start | bytes 786440 | tf_op jit(solution)/shard_map/ppermute | solution.py:327
  87.2 11.5 %collective-permute-start.9 = (bf16[512,256]{1,0:T(8,128)(2,1)}, bf16[512,256]{1,0:T(8,128)(2,1)S(1)}, u32[]{:S(2)}, u32[]{:S(2)}) collective-permute-start(bf16[512,256]{1,0:T(8,128)(2,1)} %get-tuple-element.22), channel_id=1, source_target_pairs={{0,2},{1,3},{2,0},{3,1},{4,6},{5,7},{6,4},{7,5},{8,10},{9,11},{10,... | collective-permute-start | bytes 786440 | tf_op jit(solution)/shard_map/ppermute | solution.py:327
  88.4 10.2 %collective-permute-start.10 = (bf16[512,256]{1,0:T(8,128)(2,1)}, bf16[512,256]{1,0:T(8,128)(2,1)S(1)}, u32[]{:S(2)}, u32[]{:S(2)}) collective-permute-start(bf16[512,256]{1,0:T(8,128)(2,1)} %get-tuple-element.23), channel_id=1, source_target_pairs={{0,3},{1,2},{2,1},{3,0},{4,7},{5,6},{6,5},{7,4},{8,11},{9,10},{10,... | collective-permute-start | bytes 786440 | tf_op jit(solution)/shard_map/ppermute | solution.py:327
  102.3 14.0 %collective-permute-start.21 = (bf16[512,2304]{1,0:T(8,128)(2,1)S(1)}, bf16[512,2304]{1,0:T(8,128)(2,1)S(1)}, u32[]{:S(2)}, u32[]{:S(2)}) collective-permute-start(bf16[512,2304]{1,0:T(8,128)(2,1)S(1)} %get-tuple-element.33), channel_id=1, source_target_pairs={{0,16},{16,0},{1,17},{17,1},{2,18},{18,2},{3,19},{19,3},{4,20},{20... | collective-permute-start | bytes 7077896 | tf_op jit(solution)/shard_map/ppermute | solution.py:388
